TPU v7x, 32 devices: a whole 2x2x4 slice. The times are simulated.
32 devices in a mesh: dp: 2 (over x), tp: 16 (over z, y, core).
Axes of the slice: x: 2, y: 2, z: 4, core: 2. Of those that a mesh axis runs over, the one named last changes fastest.
Arguments:
- token_ids: int32 [2, 2048], P('dp'), parts along dimension 0
- emb_table: bfloat16 [49152, 2048], P('tp')
- norm_gain: bfloat16 [2048], replicated
- grad_out: bfloat16 [2, 2048, 2048], P('dp', 'tp'), parts along dimension 0
Outputs:
- output 1: bfloat16 [2, 2048, 2048], P('dp', 'tp'), parts along dimension 0
- output 2: float32 [98304, 2048], P(('dp', 'tp')), parts along dimension 0
- output 3: float32 [4096], P('dp'), parts along dimension 0
There are 2 independent parts. A program takes and returns all parts, laid end to end along the dimension named above; an argument that names none is the same for every part.
All inputs are finite; a program needn't handle non-finite values.
Results may differ from a plain program's by a relative error of at most 0.0084057.
Values are sent between devices in bfloat16 or wider.
A program may use at most 1 GiB of HBM per device.

v0:
```python
import jax
import jax.numpy as jnp
from jax import lax
from jax.sharding import PartitionSpec as P

RMS_EPS = 1e-5


def norm_pass(embedded, norm_gain, grad_block):
    hidden_f32 = embedded.astype(jnp.float32)
    inv_rms = lax.rsqrt(jnp.mean(hidden_f32 * hidden_f32, axis=-1, keepdims=True) + RMS_EPS)
    x_hat = hidden_f32 * inv_rms
    normed = x_hat.astype(jnp.bfloat16) * norm_gain
    grad_f32 = grad_block.astype(jnp.float32)
    gain_part = jnp.sum(grad_f32 * x_hat, axis=(0, 1))
    grad_hat = grad_f32 * norm_gain.astype(jnp.float32)
    grad_in = (inv_rms * (grad_hat - x_hat * jnp.mean(grad_hat * x_hat, axis=-1, keepdims=True))).astype(jnp.bfloat16)
    return normed, grad_in, gain_part


def device_step(token_ids, table_block, norm_gain, grad_block):
    rows_block, hidden_size = table_block.shape
    tp_index = lax.axis_index('tp')
    local_ids = token_ids - tp_index * rows_block
    owned = (local_ids >= 0) & (local_ids < rows_block)
    looked_up = jnp.take(table_block, jnp.where(owned, local_ids, 0), axis=0)
    partial_rows = jnp.where(owned[:, :, None], looked_up, jnp.zeros((), jnp.bfloat16))
    embedded = lax.psum_scatter(partial_rows, 'tp', scatter_dimension=1, tiled=True)
    normed, grad_in, gain_part = norm_pass(embedded, norm_gain, grad_block)
    grad_gain = lax.psum(gain_part, 'tp')
    grad_all = lax.all_gather(grad_in, 'tp', axis=1, tiled=True)
    segment_ids = jnp.where(owned, local_ids, rows_block).reshape(-1)
    grad_table = jax.ops.segment_sum(grad_all.astype(jnp.float32).reshape(-1, hidden_size), segment_ids, num_segments=rows_block)
    return normed, grad_table, grad_gain


def solution(mesh):
    return jax.shard_map(device_step, mesh=mesh, in_specs=(P('dp', None), P('tp', None), P(None), P('dp', 'tp', None)), out_specs=(P('dp', 'tp', None), P(('dp', 'tp'), None), P('dp')), check_vma=False)
```

profile of v0, /device:TPU:9, one launch (start us, length us, event | category | flops | bytes accessed | tf_op | source)
XLA Modules:
  0.0 266.9 jit_solution(8646484640703041013)
XLA Ops:
  7.2 0.0 reduce-scatter.2.cloned.1.call-start
  7.2 0.8 and_reduce_fusion
  8.0 22.5 %gather_fusion = bf16[2048,2048]{1,0:T(8,128)(2,1)} fusion(bf16[3072,2048]{1,0:T(8,128)(2,1)} %param.5, s32[2048]{0:T(1024)S(1)} %broadcast_clamp_fusion), kind=kCustom, calls=%fused_computation | custom fusion | bytes 16785408 | tf_op jit(solution)/shard_map/jit(_take)/gather | solution.py:26
  30.5 7.7 %fusion.4 = bf16[1,2048,2048]{2,1,0:T(8,128)(2,1)} fusion(bf16[2048,2048]{1,0:T(8,128)(2,1)} %gather_fusion, pred[2048]{0:T(1024)(128)(4,1)S(1)} %get-tuple-element.5, pred[2048]{0:T(1024)(128)(4,1)S(1)} %get-tuple-element.7), kind=kLoop, calls=%fused_computation.7 | loop fusion | flops 8388608 | bytes 16781312 | tf_op jit(solution)/shard_map/jit(_where)/select_n | solution.py:27
  38.2 0.0 copy-start.2
  38.3 0.0 copy-start
  38.3 0.0 copy-start.1
  38.3 0.0 reduce-scatter.2.cloned.1.call-update
  38.3 0.0 all-gather.2.cloned.1.call-start
  38.3 0.6 copy-done.2
  38.9 103.0 %reduce-scatter.2.cloned.1.call-done = bf16[1,128,2048]{2,1,0:T(8,128)(2,1)} async-done(((bf16[1,2048,2048]{2,1,0:T(8,128)(2,1)}), bf16[1,128,2048]{2,1,0:T(8,128)(2,1)}) %reduce-scatter.2.cloned.1.call-update) | async-done | bytes 524304 | tf_op jit(solution)/shard_map/reduce_scatter | solution.py:28
  141.9 1.2 fusion.12
  143.2 0.0 copy-done
  143.2 1.5 fusion.13
  144.6 2.2 fusion.10
  146.8 0.0 all-gather.2.cloned.1.call-update
  146.9 0.0 copy-done.1
  146.9 26.1 %psum.7 = f32[2048]{0:T(1024)} all-reduce(f32[2048]{0:T(1024)S(1)} %get-tuple-element.3), channel_id=1, replica_groups=mesh['dp'=2,'tp'=16] {'tp'}, use_global_device_ids=true, to_apply=%region_5.6 | all-reduce | flops 2048 | bytes 16384 | tf_op jit(solution)/shard_map/psum | solution.py:30
  173.0 2.0 fusion.14
  175.1 46.9 %all-gather.2.cloned.1.call-done = bf16[1,2048,2048]{2,1,0:T(8,128)(2,1)} async-done(((bf16[1,128,2048]{2,1,0:T(8,128)(2,1)}), bf16[1,2048,2048]{2,1,0:T(8,128)(2,1)}) %all-gather.2.cloned.1.call-update) | async-done | bytes 8388624 | tf_op jit(solution)/shard_map/all_gather | solution.py:31
  221.9 38.1 %scatter_custom_fusion = f32[3072,2048]{1,0:T(8,128)} fusion(s32[2048]{0:T(1024)S(1)} %bitcast.13, f32[]{:T(128)} %constant.15.clone.1, bf16[1,2048,2048]{2,1,0:T(8,128)(2,1)} %all-gather.2.cloned.1.call-done), kind=kCustom, calls=%fused_computation.2 | custom fusion | flops 8388608 | bytes 33554436 | tf_op jit(solution)/shard_map/scatter-add | solution.py:33
  (5 shorter events, 0.0 us)
Async XLA Ops:
  7.2 134.8 %reduce-scatter.2.cloned.1.call-start = ((), (), s32[]{:S(2)}) async-start(), calls=%async_computation.1 | async-start | bytes 8912896 | tf_op jit(solution)/shard_map/reduce_scatter | solution.py:28
  38.2 0.7 copy-start.2
  38.3 104.9 %copy-start = (bf16[1,128,2048]{2,1,0:T(8,128)(2,1)S(1)}, bf16[1,128,2048]{2,1,0:T(8,128)(2,1)}, u32[]{:S(2)}) copy-start(bf16[1,128,2048]{2,1,0:T(8,128)(2,1)} %param.7) | copy-start | bytes 1572868
  38.3 108.6 %copy-start.1 = (s32[1,2048]{1,0:T(1,128)S(1)}, s32[1,2048]{1,0:T(1,128)}, u32[]{:S(2)}) copy-start(s32[1,2048]{1,0:T(1,128)} %param.4) | copy-start | bytes 24580
  38.3 183.7 %all-gather.2.cloned.1.call-start = ((), (), s32[]{:S(2)}) async-start(), calls=%async_computation.2 | async-start | bytes 8912896 | tf_op jit(solution)/shard_map/all_gather | solution.py:31
Sparse Core Ops, SparseCore 0:
  38.4 103.4 reduce-scatter.1
  147.0 74.8 all-gather.1
where the time goes:
time: 269 us; the launch traced here: 267 us
  waiting for transfers between devices  150 us (56%)
  other arithmetic  53.6 us (20%)
  blocking collectives  26.1 us (10%)
  local copies, waits for them, and re-layouts  23.1 us (9%)
  between operations  14.1 us (5%)
    reduce_scatter x1, waiting for transfers between devices, device_step(): lax.psum_scatter(partial_rows, 'tp', scatter_dimension=1, tiled=True)  103 us
    all_gather x1, waiting for transfers between devices, device_step(): grad_all = lax.all_gather(grad_in, 'tp', axis=1, tiled=True)  46.9 us
    scatter-add x1, other arithmetic, device_step(): jax.ops.segment_sum(grad_all.astype(jnp.float32).reshape(-1, hidden_size)...  38.1 us
    psum x1, blocking collectives, device_step(): grad_gain = lax.psum(gain_part, 'tp')  26.1 us
    gather x1, local copies, waits for them, and re-layouts, device_step(): looked_up = jnp.take(table_block, jnp.where(owned, local_ids, 0), axis=0)  22.5 us
    select_n x1, other arithmetic, device_step(): jnp.where(owned[:, :, None], looked_up, jnp.zeros((), jnp.bfloat16))  7.74 us
  transfers between devices with their start and end apart: 2, of which 2 were waited for; matrix products, arithmetic and copies ran while one was open for 1% of the time, Pallas kernels for 0%

commit v1 on v0

v1 whole, which is shorter than its diff:
```python
import functools

import jax
import jax.numpy as jnp
from jax import lax
from jax.experimental import pallas as pl
from jax.experimental.pallas import tpu as pltpu
from jax.sharding import PartitionSpec as P

RMS_EPS = 1e-5
TP = 16
ROWS = 3072
HID = 2048
SEQ = 2048
TOK = 128
XC = 32
DC = 64
NC = 512
CHUNKS = 6
MESH = pl.DeviceIdType.MESH
F32 = jnp.float32
BF16 = jnp.bfloat16
I32 = jnp.int32


def dot(a, b):
    return lax.dot_general(a, b, (((1,), (0,)), ((), ())), preferred_element_type=F32)


def one_hot(mask):
    return jnp.where(mask, 1.0, 0.0).astype(BF16)


def owner_of(ids):
    return ((ids >> 10) * 171) >> 9


def columns(rows):
    pad = jnp.zeros((128 - rows.shape[0], 128), rows.dtype)
    return jnp.concatenate([rows, pad], axis=0).T


def exchange_kernel(
    ids_ref, table_ref, gain_ref, grad_ref,
    dxc_ref, clid_ref, ys_ref, ydst_ref, dgp_ref, flag_ref,
    tbl, tbl_sem, xs, xrecv, ds, drecv, dgs, xid_s,
    xz_send, xf_send, x_sem, dz_send, df_send, d_sem, g_send, g_sem,
):
    me = lax.axis_index('tp')
    z = me // 4
    lane = me % 4
    y = lane // 2
    c = lane % 2
    sib = z * 4 + y * 2 + (1 - c)
    ymate = z * 4 + (1 - y) * 2 + c
    far = z * 4 + (1 - y) * 2 + (1 - c)
    zs = [z, z + 1 - 2 * (z % 2), z + 2 - 4 * (z // 2), 3 - z]

    barrier = pltpu.get_barrier_semaphore()

    def greet(i, carry):
        pl.semaphore_signal(barrier, inc=1, device_id={'tp': (me + i) % TP}, device_id_type=MESH)
        return carry

    lax.fori_loop(1, TP, greet, 0)

    part = ROWS // CHUNKS
    loads = [
        pltpu.make_async_copy(table_ref.at[pl.ds(i * part, part)], tbl.at[pl.ds(i * part, part)], tbl_sem.at[i])
        for i in range(CHUNKS)
    ]
    for load in loads:
        load.start()

    ids = ids_ref[...]
    own = owner_of(ids)
    idc = columns(ids)
    sub = lax.broadcasted_iota(I32, (128, 128), 0)
    lan = lax.broadcasted_iota(I32, (128, 128), 1)
    before = sub < lan
    dup_rows = []
    for s in range(4):
        for b in range(4):
            acc = jnp.zeros((128, 128), I32)
            row = ids[4 * s + b:4 * s + b + 1, :]
            for a in range(b + 1):
                same = idc[:, 4 * s + a:4 * s + a + 1] == row
                if a == b:
                    same = same & before
                acc = acc | jnp.where(same, 1, 0)
            dup_rows.append(jnp.max(acc, axis=0, keepdims=True))
    first = jnp.concatenate(dup_rows, axis=0) == 0
    key = jnp.where(first, own, -1)
    keyc = columns(key)
    rank_rows = []
    for s in range(4):
        for b in range(4):
            acc = jnp.zeros((128, 128), I32)
            row = own[4 * s + b:4 * s + b + 1, :]
            for a in range(b + 1):
                same = keyc[:, 4 * s + a:4 * s + a + 1] == row
                if a == b:
                    same = same & before
                acc = acc + jnp.where(same, 1, 0)
            rank_rows.append(jnp.sum(acc, axis=0, keepdims=True))
    rank = jnp.concatenate(rank_rows, axis=0)

    local = ids - me * ROWS
    mine = own == me
    xslot = jnp.where(first & mine, rank, -1)
    slot_iota = lax.broadcasted_iota(I32, (XC, 128), 0)
    lids = []
    for s in range(4):
        acc = jnp.zeros((XC, 128), I32)
        for a in range(4):
            d = 4 * s + a
            acc = acc + jnp.where(slot_iota == xslot[d:d + 1, :], local[d:d + 1, :] + 1, 0)
        lids.append(jnp.sum(acc, axis=1, keepdims=True) - 1)
    lid = jnp.concatenate(lids, axis=0)

    packed = jnp.zeros((4 * XC, HID), F32)
    chunk_iota = lax.broadcasted_iota(I32, (4 * XC, part), 1)
    for i in range(CHUNKS):
        loads[i].wait()
        packed = packed + dot(one_hot(chunk_iota + i * part == lid), tbl[pl.ds(i * part, part), :])
    packed = packed.astype(BF16)
    for s in range(4):
        xs[s] = packed[s * XC:(s + 1) * XC, :]
    xrecv[me] = xs[z]

    pl.semaphore_wait(barrier, TP - 1)

    def send(src, dst, ssem, rsem, dev):
        cp = pltpu.make_async_remote_copy(
            src_ref=src, dst_ref=dst, send_sem=ssem, recv_sem=rsem, device_id={'tp': dev}, device_id_type=MESH)
        cp.start()
        return cp

    sends = []

    def arrive(buf, sem, src):
        pltpu.make_async_remote_copy(
            src_ref=buf.at[src], dst_ref=buf.at[src], send_sem=xz_send.at[0], recv_sem=sem.at[src],
            device_id={'tp': sib}, device_id_type=MESH).wait_recv()

    def forward_own(buf, ssem, sem, k):
        src = zs[k] * 4 + lane
        if k:
            arrive(buf, sem, src)
        sends.append(send(buf.at[src], buf.at[src], ssem.at[3 * k], sem.at[src], ymate))
        sends.append(send(buf.at[src], buf.at[src], ssem.at[3 * k + 1], sem.at[src], sib))

    def forward_mate(buf, ssem, sem, k):
        src = zs[k] * 4 + (1 - y) * 2 + c
        arrive(buf, sem, src)
        sends.append(send(buf.at[src], buf.at[src], ssem.at[3 * k + 2], sem.at[src], sib))

    def collect(buf, sem, k):
        arrive(buf, sem, zs[k] * 4 + y * 2 + (1 - c))
        arrive(buf, sem, zs[k] * 4 + (1 - y) * 2 + (1 - c))

    for k in range(1, 4):
        sends.append(send(xs.at[zs[k]], xrecv.at[me], xz_send.at[k - 1], x_sem.at[me], zs[k] * 4 + lane))
    forward_own(xrecv, xf_send, x_sem, 0)

    xall = jnp.where(first, own * XC + rank, -1)
    over = jnp.max(jnp.where(first & (rank >= XC), 1, 0))

    def slab(rows):
        out = jnp.zeros((4, 128), I32)
        for s in range(4):
            out = out + jnp.where(z == s, rows[4 * s:4 * s + 4, :], 0)
        return out

    tslot = jnp.where(slab(jnp.where(first, 1, 0)) == 1, slab(jnp.where(rank < XC, xall, -1)), -1)
    mine_c = columns(jnp.concatenate([tslot, slab(ids)], axis=0))
    for q in range(4):
        acc = jnp.zeros((128, 128), I32)
        for a in range(4):
            acc = acc + jnp.where(mine_c[:, a:a + 1] == lan + q * 128, mine_c[:, 4 + a:5 + a] + 1, 0)
        xid_s[q:q + 1, :] = jnp.sum(acc, axis=0, keepdims=True) - 1

    zown = own >> 2
    zc = ((idc >> 10) * 171) >> 11
    drank_rows = []
    for d in range(TP):
        same = (zc[:, d:d + 1] == zown[d:d + 1, :]) & before
        drank_rows.append(jnp.sum(jnp.where(same, 1, 0), axis=0, keepdims=True))
    drank = jnp.concatenate(drank_rows, axis=0)
    over = jnp.maximum(over, jnp.max(jnp.where(drank >= DC, 1, 0)))
    row_iota = lax.broadcasted_iota(I32, (TP, 128), 0)

    def my_row(rows):
        return jnp.sum(jnp.where(row_iota == me, rows, 0), axis=0, keepdims=True)

    my_ids, my_rank, my_zown = my_row(ids), my_row(drank), my_row(zown)
    ydst_ref[...] = jnp.broadcast_to(my_zown * DC + my_rank, (8, 128))
    dslot_iota = lax.broadcasted_iota(I32, (DC, 128), 0)
    gain = gain_ref[...]
    gain_f = gain.astype(F32)
    gain_sum = jnp.zeros((1, HID), F32)

    forward_mate(xrecv, xf_send, x_sem, 0)
    for k in range(4):
        if k < 3:
            forward_own(xrecv, xf_send, x_sem, k + 1)
        collect(xrecv, x_sem, k)
        zk = zs[k]
        pick = (dslot_iota == my_rank) & (my_zown == zk)
        did = jnp.sum(jnp.where(pick, my_ids + 1, 0), axis=1, keepdims=True) - 1
        xid = xid_s[pl.ds(zk, 1), :]
        from_recv = one_hot((did == xid) & (did >= 0))
        h_all = dot(from_recv, jnp.concatenate([xrecv[zk * 4 + j] for j in range(4)], axis=0))
        g_all = dot(one_hot(pick), grad_ref[...])
        dst = me if k == 0 else zk
        for r0 in range(0, DC, 16):
            h = h_all[r0:r0 + 16, :]
            inv = lax.rsqrt(jnp.mean(h * h, axis=-1, keepdims=True) + RMS_EPS)
            xh = h * inv
            gr = g_all[r0:r0 + 16, :]
            gain_sum = gain_sum + jnp.sum(gr * xh, axis=0, keepdims=True)
            u = gr * gain_f
            dx = inv * (u - xh * jnp.mean(u * xh, axis=-1, keepdims=True))
            ys_ref[zk, pl.ds(r0, 16), :] = xh.astype(BF16) * gain
            if k == 0:
                drecv[me, pl.ds(r0, 16), :] = dx.astype(BF16)
            else:
                ds[k - 1, pl.ds(r0, 16), :] = dx.astype(BF16)
        if k:
            sends.append(send(ds.at[k - 1], drecv.at[me], dz_send.at[k - 1], d_sem.at[me], zk * 4 + lane))
        else:
            forward_own(drecv, df_send, d_sem, 0)
        if k < 3:
            forward_mate(xrecv, xf_send, x_sem, k + 1)
        else:
            forward_mate(drecv, df_send, d_sem, 0)

    dgs[...] = gain_sum
    dgp_ref[me] = gain_sum
    for i in range(1, TP):
        sends.append(send(dgs, dgp_ref.at[me], g_send.at[i - 1], g_sem.at[me], (me + i) % TP))

    dslot = jnp.where(mine & (drank < DC), drank, -1)
    dslot_c = columns(dslot)
    lrows = []
    for p in range(8):
        acc = jnp.zeros((128, 128), I32)
        for j in range(2):
            d = 2 * p + j
            sc = dslot_c[:, d:d + 1]
            acc = acc + jnp.where((sc >= 0) & (sc + 64 * j == lan), idc[:, d:d + 1] - me * ROWS + 1, 0)
        lrows.append(jnp.sum(acc, axis=0, keepdims=True))
    lid1 = jnp.concatenate(lrows, axis=0)
    has = lid1 > 0
    has_f = jnp.where(has, 1.0, 0.0)
    inrow = dot(has_f.astype(BF16), one_hot(before))
    total = jnp.sum(has_f, axis=1, keepdims=True)
    crank_rows = []
    base = jnp.zeros((1, 1), F32)
    for p in range(8):
        crank_rows.append(inrow[p:p + 1, :] + base)
        base = base + total[p:p + 1, :]
    for o in range(TP):
        over = jnp.maximum(over, jnp.where(jnp.sum(jnp.where(own == o, 1.0, 0.0)) > NC, 1, 0))
    crank = jnp.where(has, jnp.concatenate(crank_rows, axis=0).astype(I32), -1)
    n_iota = lax.broadcasted_iota(I32, (NC, 128), 0)
    compact = jnp.concatenate([one_hot(n_iota == crank[p:p + 1, :]) for p in range(8)], axis=1)
    lrow = jnp.concatenate([lid1[p:p + 1, :] for p in range(8)], axis=1)
    halves = jnp.concatenate([lrow >> 6, lrow & 63, jnp.zeros((6, TP * DC), I32)], axis=0).astype(F32).astype(BF16)
    cl = lax.dot_general(halves, compact, (((1,), (1,)), ((), ())), preferred_element_type=F32)
    clid_ref[...] = jnp.broadcast_to((cl[0:1, :] * 64.0 + cl[1:2, :]).astype(I32) - 1, (8, NC))
    flag_ref[0] = over

    for k in range(1, 4):
        forward_own(drecv, df_send, d_sem, k)
        forward_mate(drecv, df_send, d_sem, k)
    for k in range(4):
        collect(drecv, d_sem, k)
    dxc_ref[...] = dot(compact, jnp.concatenate([drecv[d] for d in range(TP)], axis=0)).astype(BF16)
    for i in range(1, TP):
        src = (me + i) % TP
        pltpu.make_async_remote_copy(
            src_ref=dgs, dst_ref=dgp_ref.at[src], send_sem=g_send.at[i - 1], recv_sem=g_sem.at[src],
            device_id={'tp': sib}, device_id_type=MESH).wait_recv()
    for cp in sends:
        cp.wait_send()


def exchange(ids, table, gain, grad):
    vmem = pl.BlockSpec(memory_space=pltpu.VMEM)
    return pl.pallas_call(
        exchange_kernel,
        out_shape=(
            jax.ShapeDtypeStruct((NC, HID), BF16),
            jax.ShapeDtypeStruct((8, NC), I32),
            jax.ShapeDtypeStruct((4, DC, HID), BF16),
            jax.ShapeDtypeStruct((8, 128), I32),
            jax.ShapeDtypeStruct((TP, 1, HID), F32),
            jax.ShapeDtypeStruct((1,), I32),
        ),
        in_specs=[vmem, pl.BlockSpec(memory_space=pl.ANY), vmem, vmem],
        out_specs=(vmem, vmem, vmem, vmem, vmem, pl.BlockSpec(memory_space=pltpu.SMEM)),
        scratch_shapes=[
            pltpu.VMEM((ROWS, HID), BF16),
            pltpu.SemaphoreType.DMA((CHUNKS,)),
            pltpu.VMEM((4, XC, HID), BF16),
            pltpu.VMEM((TP, XC, HID), BF16),
            pltpu.VMEM((3, DC, HID), BF16),
            pltpu.VMEM((TP, DC, HID), BF16),
            pltpu.VMEM((1, HID), F32),
            pltpu.VMEM((8, 128), I32),
            pltpu.SemaphoreType.DMA((3,)),
            pltpu.SemaphoreType.DMA((12,)),
            pltpu.SemaphoreType.DMA((TP,)),
            pltpu.SemaphoreType.DMA((3,)),
            pltpu.SemaphoreType.DMA((12,)),
            pltpu.SemaphoreType.DMA((TP,)),
            pltpu.SemaphoreType.DMA((TP - 1,)),
            pltpu.SemaphoreType.DMA((TP,)),
        ],
        compiler_params=pltpu.CompilerParams(collective_id=0, has_side_effects=True),
        name='exchange',
    )(ids, table, gain, grad)


BLK = 128


def finish_kernel(dxc_ref, clid_ref, ys_ref, ydst_ref, dgp_ref, de_ref, y_ref, dg_ref):
    i = pl.program_id(0)
    rows = lax.broadcasted_iota(I32, (BLK, NC), 0) + i * BLK
    de_ref[...] = dot(one_hot(rows == clid_ref[0:1, :]), dxc_ref[...])

    @pl.when(i == 0)
    def _():
        spread = one_hot(lax.broadcasted_iota(I32, (4 * DC, 128), 0) == ydst_ref[0:1, :])
        ys = jnp.concatenate([ys_ref[s] for s in range(4)], axis=0)
        y_ref[...] = lax.dot_general(spread, ys, (((0,), (0,)), ((), ())), preferred_element_type=F32).astype(BF16)
        total = dgp_ref[0]
        for d in range(1, TP):
            total = total + dgp_ref[d]
        dg_ref[...] = total


def finish(dxc, clid, ys, ydst, dgp):
    def whole(shape):
        return pl.BlockSpec(shape, lambda i: (0,) * len(shape))

    return pl.pallas_call(
        finish_kernel,
        grid=(ROWS // BLK,),
        out_shape=(
            jax.ShapeDtypeStruct((ROWS, HID), F32),
            jax.ShapeDtypeStruct((TOK, HID), BF16),
            jax.ShapeDtypeStruct((1, HID), F32),
        ),
        in_specs=[whole((NC, HID)), whole((8, NC)), whole((4, DC, HID)), whole((8, 128)), whole((TP, 1, HID))],
        out_specs=(pl.BlockSpec((BLK, HID), lambda i: (i, 0)), whole((TOK, HID)), whole((1, HID))),
        name='finish',
    )(dxc, clid, ys, ydst, dgp)


def swap_kernel(src_ref, dst_ref, local_sem, send_sem, recv_sem):
    me = lax.axis_index('tp')
    barrier = pltpu.get_barrier_semaphore()

    def greet(i, carry):
        pl.semaphore_signal(barrier, inc=1, device_id={'tp': (me + i) % TP}, device_id_type=MESH)
        return carry

    lax.fori_loop(1, TP, greet, 0)
    pl.semaphore_wait(barrier, TP - 1)

    def copy(i):
        peer = (me + i) % TP
        return pltpu.make_async_remote_copy(
            src_ref=src_ref.at[peer], dst_ref=dst_ref.at[me], send_sem=send_sem.at[i], recv_sem=recv_sem.at[me],
            device_id={'tp': peer}, device_id_type=MESH)

    def start(i, carry):
        copy(i).start()
        return carry

    lax.fori_loop(1, TP, start, 0)
    keep = pltpu.make_async_copy(src_ref.at[me], dst_ref.at[me], local_sem)
    keep.start()

    def wait(i, carry):
        peer = (me + i) % TP
        pltpu.make_async_remote_copy(
            src_ref=src_ref.at[peer], dst_ref=dst_ref.at[peer], send_sem=send_sem.at[i], recv_sem=recv_sem.at[peer],
            device_id={'tp': peer}, device_id_type=MESH).wait()
        return carry

    lax.fori_loop(1, TP, wait, 0)
    keep.wait()


def swap(blocks, cid):
    return pl.pallas_call(
        swap_kernel,
        out_shape=jax.ShapeDtypeStruct(blocks.shape, blocks.dtype),
        in_specs=[pl.BlockSpec(memory_space=pl.ANY)],
        out_specs=pl.BlockSpec(memory_space=pl.ANY),
        scratch_shapes=[pltpu.SemaphoreType.DMA, pltpu.SemaphoreType.DMA((TP,)), pltpu.SemaphoreType.DMA((TP,))],
        compiler_params=pltpu.CompilerParams(collective_id=cid, has_side_effects=True),
        name='swap',
    )(blocks)


def general(ids, table, gain, grad):
    local = ids.reshape(-1) - lax.axis_index('tp') * ROWS
    mine = (local >= 0) & (local < ROWS)
    looked = jnp.take(table, jnp.where(mine, local, 0), axis=0)
    parts = swap(jnp.where(mine[:, None], looked, jnp.zeros((), BF16)).reshape(TP, TOK, HID), 1)
    h = jnp.sum(parts.astype(F32), axis=0)
    inv = lax.rsqrt(jnp.mean(h * h, axis=-1, keepdims=True) + RMS_EPS)
    xh = h * inv
    y = xh.astype(BF16) * gain
    gr = grad.astype(F32)
    part = jnp.sum(gr * xh, axis=0)
    u = gr * gain.astype(F32)
    dx = (inv * (u - xh * jnp.mean(u * xh, axis=-1, keepdims=True))).astype(BF16)
    dx_all = swap(jnp.broadcast_to(dx[None], (TP, TOK, HID)), 2).reshape(SEQ, HID)
    dg = jnp.sum(swap(jnp.broadcast_to(part.reshape(1, TOK // 8, 128), (TP, TOK // 8, 128)), 3), axis=0).reshape(1, HID)
    de = jax.ops.segment_sum(dx_all.astype(F32), jnp.where(mine, local, ROWS), num_segments=ROWS)
    return de, y, dg


def device_step(token_ids, table, gain, grad):
    ids = token_ids.reshape(TP, TOK)
    gain = gain.reshape(1, HID)
    grad = grad.reshape(TOK, HID)
    dxc, clid, ys, ydst, dgp, flag = exchange(ids, table, gain, grad)
    de, y, dg = lax.cond(
        flag[0] > 0,
        lambda: general(ids, table, gain, grad),
        lambda: finish(dxc, clid, ys, ydst, dgp),
    )
    return y.reshape(1, TOK, HID), de, dg.reshape(HID)


def solution(mesh):
    return jax.shard_map(
        device_step, mesh=mesh,
        in_specs=(P('dp', None), P('tp', None), P(None), P('dp', 'tp', None)),
        out_specs=(P('dp', 'tp', None), P(('dp', 'tp'), None), P('dp')), check_vma=False)
```

time: 269 us -> 93.1 us (0.35)
  the two profiles are of different devices: /device:TPU:9 before, /device:TPU:1 now
where the time goes in v1:
time: 93.1 us; the launch traced here: 92.8 us
  Pallas kernels  89.9 us (97%)
  local copies, waits for them, and re-layouts  1.56 us (2%)
  between operations  1.36 us (1%)
    pallas_call x1, Pallas kernels, exchange(): pl.pallas_call(exchange_kernel, out_shape=(jax.ShapeDtypeStruct((NC, HID)...  70.4 us
    pallas_call x1, Pallas kernels, finish(): pl.pallas_call(finish_kernel, grid=(ROWS // BLK,), out_shape=(jax.ShapeDt...  19.5 us

profile of v1, /device:TPU:1, one launch (start us, length us, event | category | flops | bytes accessed | tf_op | source)
XLA Modules:
  0.0 92.8 jit_solution(16664040165600102368)
XLA Ops:
  0.6 0.0 copy-start.1
  0.6 0.0 copy-start
  0.7 0.8 reshape.154.gain_ref
  1.4 70.4 %exchange.1 = (bf16[512,2048]{1,0:T(8,128)(2,1)}, s32[8,512]{1,0:T(8,128)S(1)}, bf16[4,64,2048]{2,1,0:T(8,128)(2,1)S(1)}, s32[8,128]{1,0:T(8,128)S(1)}, f32[16,1,2048]{2,1,0:T(1,128)S(1)}, /*index=5*/s32[1]{0:T(128)}) custom-call(s32[16,128]{1,0:T(8,128)} %bitcast.27, bf16[3072,2048]{1,0:T(8,128)(2,1)} %table_ref.1, bf16[1,2048]{1,0:T(2,128)(2,1)S(1)} %reshape.154.gain_ref, ...), custom_call_target="tpu_custom_call" | custom-call | tf_op jit(solution)/shard_map/exchange/pallas_call | solution.py:291
  72.5 0.0 copy-done.1
  72.5 0.0 copy-done
  72.5 19.5 %conditional.1 = (f32[3072,2048]{1,0:T(8,128)}, bf16[1,128,2048]{2,1,0:T(8,128)(2,1)S(1)}, f32[2048]{0:T(1024)S(1)}) conditional(s32[]{:T(128)} %bitcast.14, (bf16[512,2048]{1,0:T(8,128)(2,1)}, s32[8,512]{1,0:T(8,128)S(1)}, bf16[4,64,2048]{2,1,0:T(8,128)(2,1)S(1)}, s32[8,128]{1,0:T(8,128)S(1)}, f32[16,1,2048]{2,1,0:T(1,128)S(1)}) %tuple.20, ...), branch_computations={%region_0.0_spmd, %region_1.8_spmd} | conditional | flops 29962372 | bytes 92165192 | solution.py:435
  72.5 19.5 %finish.1 = (f32[3072,2048]{1,0:T(8,128)}, bf16[128,2048]{1,0:T(8,128)(2,1)S(1)}, f32[1,2048]{1,0:T(1,128)S(1)}) custom-call(bf16[512,2048]{1,0:T(8,128)(2,1)} %get-tuple-element.23.dxc_ref, s32[8,512]{1,0:T(8,128)S(1)} %get-tuple-element.24.clid_ref, bf16[4,64,2048]{2,1,0:T(8,128)(2,1)S(1)} %get-tuple-element.25.ys_ref, ...), custom_call_target="tpu_custom_call" | custom-call | tf_op jit(solution)/shard_map/cond/branch_0_fun/finish/pallas_call | solution.py:349
  92.0 0.0 copy-start.2
  92.0 0.0 copy-start.3
  92.0 0.8 copy-done.2
  92.8 0.0 copy-done.3
Async XLA Ops:
  0.6 71.9 %copy-start.1 = (s32[1,2048]{1,0:T(1,128)S(1)}, s32[1,2048]{1,0:T(1,128)}, u32[]{:S(2)}) copy-start(s32[1,2048]{1,0:T(1,128)} %param.6) | copy-start | bytes 24580
  0.6 71.9 %copy-start = (bf16[1,128,2048]{2,1,0:T(8,128)(2,1)S(1)}, bf16[1,128,2048]{2,1,0:T(8,128)(2,1)}, u32[]{:S(2)}) copy-start(bf16[1,128,2048]{2,1,0:T(8,128)(2,1)} %param.9) | copy-start | bytes 1572868
  92.0 0.8 copy-start.2
  92.0 0.8 copy-start.3

commit v2 on v1

v2 whole, which is shorter than its diff:
```python
import functools

import jax
import jax.numpy as jnp
from jax import lax
from jax.experimental import pallas as pl
from jax.experimental.pallas import tpu as pltpu
from jax.sharding import PartitionSpec as P

RMS_EPS = 1e-5
TP = 16
ROWS = 3072
HID = 2048
SEQ = 2048
TOK = 128
XC = 32
DC = 56
DW = 40
NC = 512
CHUNKS = 6
MESH = pl.DeviceIdType.MESH
F32 = jnp.float32
BF16 = jnp.bfloat16
I32 = jnp.int32


def dot(a, b):
    return lax.dot_general(a, b, (((1,), (0,)), ((), ())), preferred_element_type=F32)


def one_hot(mask):
    return jnp.where(mask, 1.0, 0.0).astype(BF16)


def owner_of(ids):
    return ((ids >> 10) * 171) >> 9


def columns(rows):
    pad = jnp.zeros((128 - rows.shape[0], 128), rows.dtype)
    return jnp.concatenate([rows, pad], axis=0).T


def exchange_kernel(
    ids_ref, table_ref, gain_ref, grad_ref,
    dxc_ref, clid_ref, y_ref, dgp_ref, flag_ref,
    tbl, tbl_sem, xs, xrecv, ds, zbuf, drecv, dxs, dgs,
    xz_send, xf_send, x_sem, dz_send, z_sem, df_send, d_sem, g_send, g_sem,
):
    me = lax.axis_index('tp')
    z = me // 4
    lane = me % 4
    y = lane // 2
    c = lane % 2
    sib = z * 4 + y * 2 + (1 - c)
    ymate = z * 4 + (1 - y) * 2 + c
    zs = [z, z + 1 - 2 * (z % 2), z + 2 - 4 * (z // 2), 3 - z]

    barrier = pltpu.get_barrier_semaphore()

    def greet(i, carry):
        pl.semaphore_signal(barrier, inc=1, device_id={'tp': (me + i) % TP}, device_id_type=MESH)
        return carry

    lax.fori_loop(1, TP, greet, 0)

    part = ROWS // CHUNKS
    loads = [
        pltpu.make_async_copy(table_ref.at[pl.ds(i * part, part)], tbl.at[pl.ds(i * part, part)], tbl_sem.at[i])
        for i in range(CHUNKS)
    ]
    for load in loads:
        load.start()

    sends = []

    def send(src, dst, ssem, rsem, dev):
        cp = pltpu.make_async_remote_copy(
            src_ref=src, dst_ref=dst, send_sem=ssem, recv_sem=rsem, device_id={'tp': dev}, device_id_type=MESH)
        cp.start()
        sends.append(cp)

    def arrived(ref, sem):
        pltpu.make_async_remote_copy(
            src_ref=ref, dst_ref=ref, send_sem=xz_send.at[0], recv_sem=sem,
            device_id={'tp': sib}, device_id_type=MESH).wait_recv()

    ids = ids_ref[...]
    own = owner_of(ids)
    row_iota = lax.broadcasted_iota(I32, (TP, 128), 0)
    sub = lax.broadcasted_iota(I32, (128, 128), 0)
    lan = lax.broadcasted_iota(I32, (128, 128), 1)
    before = sub < lan

    def my_row(rows):
        return jnp.sum(jnp.where(row_iota == me, rows, 0), axis=0, keepdims=True)

    my_own = my_row(own)
    my_own_c = columns(jnp.broadcast_to(my_own, (8, 128)))[:, 0:1]
    my_chip = my_own >> 1
    same = ((my_own_c >> 1) == my_chip) & before
    my_rank = jnp.sum(jnp.where(same, 1, 0), axis=0, keepdims=True)
    my_slot = jnp.where((my_chip & 1) == 0, my_rank, DC - 1 - my_rank)
    my_zown = my_own >> 2
    dslot_iota = lax.broadcasted_iota(I32, (DC, 128), 0)

    def pack_dy(k):
        pick = (dslot_iota == my_slot) & (my_zown == zs[k])
        return dot(one_hot(pick), grad_ref[...]).astype(BF16)

    lo, hi = y * (DC - DW), (1 - y) * (DC - DW)

    def forward_z(k):
        src = zs[k] * 4 + lane
        if k:
            arrived(zbuf.at[k], z_sem.at[k])
        send(zbuf.at[k, pl.ds(pl.multiple_of(hi, 8), DW)], drecv.at[src], df_send.at[3 * k], d_sem.at[src], ymate)
        send(zbuf.at[k, pl.ds(pl.multiple_of(lo, 8), DW)], drecv.at[src], df_send.at[3 * k + 1], d_sem.at[src], sib)

    def forward_zmate(k):
        src = zs[k] * 4 + (1 - y) * 2 + c
        arrived(drecv.at[src], d_sem.at[src])
        send(drecv.at[src], drecv.at[src], df_send.at[3 * k + 2], d_sem.at[src], sib)

    def collect_dy(k):
        for j in range(2):
            src = zs[k] * 4 + ((1 - y) * 2 if j else y * 2) + (1 - c)
            arrived(drecv.at[src], d_sem.at[src])

    for k in (1, 2, 3):
        ds[k - 1] = pack_dy(k)
    zbuf[0] = pack_dy(0)
    pl.semaphore_wait(barrier, TP - 1)
    for k in (1, 2, 3):
        send(ds.at[k - 1], zbuf.at[k], dz_send.at[k - 1], z_sem.at[k], zs[k] * 4 + lane)
    forward_z(0)

    idc = columns(ids)
    dup_rows = []
    for s in range(4):
        for b in range(4):
            acc = jnp.zeros((128, 128), I32)
            row = ids[4 * s + b:4 * s + b + 1, :]
            for a in range(b + 1):
                same = idc[:, 4 * s + a:4 * s + a + 1] == row
                if a == b:
                    same = same & before
                acc = acc | jnp.where(same, 1, 0)
            dup_rows.append(jnp.max(acc, axis=0, keepdims=True))
    first = jnp.concatenate(dup_rows, axis=0) == 0
    key = jnp.where(first, own, -1)
    keyc = columns(key)
    rank_rows = []
    for s in range(4):
        for b in range(4):
            acc = jnp.zeros((128, 128), I32)
            row = own[4 * s + b:4 * s + b + 1, :]
            for a in range(b + 1):
                same = keyc[:, 4 * s + a:4 * s + a + 1] == row
                if a == b:
                    same = same & before
                acc = acc + jnp.where(same, 1, 0)
            rank_rows.append(jnp.sum(acc, axis=0, keepdims=True))
    rank = jnp.concatenate(rank_rows, axis=0)

    local = ids - me * ROWS
    mine = own == me
    xslot = jnp.where(first & mine, rank, -1)
    slot_iota = lax.broadcasted_iota(I32, (XC, 128), 0)
    lids = []
    for s in range(4):
        acc = jnp.zeros((XC, 128), I32)
        for a in range(4):
            d = 4 * s + a
            acc = acc + jnp.where(slot_iota == xslot[d:d + 1, :], local[d:d + 1, :] + 1, 0)
        lids.append(jnp.sum(acc, axis=1, keepdims=True) - 1)
    lid = jnp.concatenate(lids, axis=0)

    packed = jnp.zeros((4 * XC, HID), F32)
    chunk_iota = lax.broadcasted_iota(I32, (4 * XC, part), 1)
    for i in range(CHUNKS):
        loads[i].wait()
        packed = packed + dot(one_hot(chunk_iota + i * part == lid), tbl[pl.ds(i * part, part), :])
    packed = packed.astype(BF16)
    for s in range(4):
        xs[s] = packed[s * XC:(s + 1) * XC, :]
    xrecv[me] = xs[z]

    def forward_x(k):
        src = zs[k] * 4 + lane
        if k:
            arrived(xrecv.at[src], x_sem.at[src])
        send(xrecv.at[src], xrecv.at[src], xf_send.at[3 * k], x_sem.at[src], ymate)
        send(xrecv.at[src], xrecv.at[src], xf_send.at[3 * k + 1], x_sem.at[src], sib)

    def forward_xmate(k):
        src = zs[k] * 4 + (1 - y) * 2 + c
        arrived(xrecv.at[src], x_sem.at[src])
        send(xrecv.at[src], xrecv.at[src], xf_send.at[3 * k + 2], x_sem.at[src], sib)

    def collect_x(k):
        for j in range(2):
            src = zs[k] * 4 + ((1 - y) * 2 if j else y * 2) + (1 - c)
            arrived(xrecv.at[src], x_sem.at[src])

    for k in (1, 2, 3):
        send(xs.at[zs[k]], xrecv.at[me], xz_send.at[k - 1], x_sem.at[me], zs[k] * 4 + lane)
    forward_x(0)
    forward_z(1)
    forward_zmate(0)

    over = jnp.max(jnp.where(first & (rank >= XC), 1, 0))

    def slab(rows):
        out = jnp.zeros((4, 128), I32)
        for s in range(4):
            out = out + jnp.where(z == s, rows[4 * s:4 * s + 4, :], 0)
        return out

    tslot = slab(jnp.where(first & (rank < XC), own * XC + rank, -1))
    mine_c = columns(jnp.concatenate([tslot, slab(ids), jnp.broadcast_to(my_row(ids), (8, 128))], axis=0))
    my_ids_c = mine_c[:, 8:9]
    spread = []
    for q in range(4):
        acc = jnp.zeros((128, 128), I32)
        for a in range(4):
            acc = acc + jnp.where(mine_c[:, a:a + 1] == lan + q * 128, mine_c[:, 4 + a:5 + a] + 1, 0)
        spread.append(one_hot(my_ids_c == jnp.sum(acc, axis=0, keepdims=True) - 1))
    spread = jnp.concatenate(spread, axis=1)

    chip_c = ((idc >> 10) * 171) >> 10
    chip = own >> 1
    drank_rows = []
    for d in range(TP):
        same = (chip_c[:, d:d + 1] == chip[d:d + 1, :]) & before
        drank_rows.append(jnp.sum(jnp.where(same, 1, 0), axis=0, keepdims=True))
    drank = jnp.concatenate(drank_rows, axis=0)
    over = jnp.maximum(over, jnp.max(jnp.where(drank >= DW, 1, 0)))
    for s in range(4):
        in_slab = jnp.sum(jnp.where((own >> 2) == s, 1.0, 0.0), axis=1, keepdims=True)
        over = jnp.maximum(over, jnp.max(jnp.where(in_slab > DC, 1, 0)))
    for o in range(TP):
        over = jnp.maximum(over, jnp.where(jnp.sum(jnp.where(own == o, 1.0, 0.0)) > NC, 1, 0))
    flag_ref[0] = over
    forward_xmate(0)

    dslot = jnp.where(mine & (drank < DW), jnp.where(y == 0, drank, DW - 1 - drank), -1)
    dslot_c = columns(dslot)
    lrows = []
    for p in range(TP * DW // 128):
        acc = jnp.zeros((128, 128), I32)
        for d in range(TP):
            if d * DW < (p + 1) * 128 and (d + 1) * DW > p * 128:
                sc = dslot_c[:, d:d + 1]
                acc = acc + jnp.where((sc >= 0) & (sc + (d * DW - p * 128) == lan), idc[:, d:d + 1] - me * ROWS + 1, 0)
        lrows.append(jnp.sum(acc, axis=0, keepdims=True))
    lid1 = jnp.concatenate(lrows + [jnp.zeros((8 - len(lrows), 128), I32)], axis=0)
    has = lid1 > 0
    has_f = jnp.where(has, 1.0, 0.0)
    inrow = dot(has_f.astype(BF16), one_hot(before))
    total = jnp.sum(has_f, axis=1, keepdims=True)
    crank_rows = []
    base = jnp.zeros((1, 1), F32)
    for p in range(8):
        crank_rows.append(inrow[p:p + 1, :] + base)
        base = base + total[p:p + 1, :]
    crank = jnp.where(has, jnp.concatenate(crank_rows, axis=0).astype(I32), -1)
    n_iota = lax.broadcasted_iota(I32, (NC, 128), 0)
    compact = jnp.concatenate([one_hot(n_iota == crank[p:p + 1, :]) for p in range(len(lrows))], axis=1)
    lrow = jnp.concatenate([lid1[p:p + 1, :] for p in range(len(lrows))], axis=1)
    halves = jnp.concatenate([lrow >> 6, lrow & 63, jnp.zeros((6, TP * DW), I32)], axis=0).astype(F32).astype(BF16)
    cl = lax.dot_general(halves, compact, (((1,), (1,)), ((), ())), preferred_element_type=F32)
    clid_ref[...] = jnp.broadcast_to((cl[0:1, :] * 64.0 + cl[1:2, :]).astype(I32) - 1, (8, NC))

    gain = gain_ref[...]
    gain_f = gain.astype(F32)
    xlid = jnp.broadcast_to(lid, (4 * XC, 128)).T[0:1, :]
    w_iota = lax.broadcasted_iota(I32, (DW, 128), 0)
    x_group = lax.broadcasted_iota(I32, (1, 4 * XC), 1) // XC

    steps = [(r0, min(16, DW - r0)) for r0 in range(0, DW, 16)]

    def dx_rows(zk, dy_of, gain_sum):
        pick_row = jnp.where(x_group == zk, xlid, -2)
        for block, at in dy_of:
            slot_row = jnp.sum(jnp.where(row_iota == at, dslot, 0), axis=0, keepdims=True)
            local_row = jnp.sum(jnp.where(row_iota == at, local, 0), axis=0, keepdims=True)
            dlid = jnp.sum(jnp.where(w_iota == slot_row, local_row + 1, 0), axis=1, keepdims=True) - 1
            h_all = dot(one_hot(dlid == pick_row), jnp.concatenate([xs[s] for s in range(4)], axis=0))
            for r0, n in steps:
                h = h_all[r0:r0 + n, :]
                inv = lax.rsqrt(jnp.mean(h * h, axis=-1, keepdims=True) + RMS_EPS)
                xh = h * inv
                gr = block(r0, n).astype(F32)
                gain_sum = gain_sum + jnp.sum(gr * xh, axis=0, keepdims=True)
                u = gr * gain_f
                dx = inv * (u - xh * jnp.mean(u * xh, axis=-1, keepdims=True))
                dxs[at, pl.ds(r0, n), :] = dx.astype(BF16)
        return gain_sum

    def process(k, gain_sum):
        collect_dy(k)
        zk = zs[k]
        out = [(lambda r0, n: zbuf[k, pl.ds(pl.multiple_of(lo + r0, 8), n), :], zk * 4 + lane)]
        for off in ((1 - y) * 2 + c, y * 2 + (1 - c), (1 - y) * 2 + (1 - c)):
            at = zk * 4 + off
            out.append((lambda r0, n, at=at: drecv[at, pl.ds(r0, n), :], at))
        return dx_rows(zk, out, gain_sum)

    forward_z(2)
    forward_zmate(1)
    gain_sum = process(0, jnp.zeros((1, HID), F32))
    forward_z(3)
    forward_zmate(2)
    gain_sum = process(1, gain_sum)
    forward_x(1)
    forward_zmate(3)
    gain_sum = process(2, gain_sum)
    forward_x(2)
    forward_xmate(1)
    gain_sum = process(3, gain_sum)
    dgs[...] = gain_sum
    dgp_ref[me] = gain_sum
    for i in range(1, TP):
        send(dgs, dgp_ref.at[me], g_send.at[i - 1], g_sem.at[me], (me + i) % TP)
    forward_x(3)
    forward_xmate(2)
    dxc_ref[...] = dot(compact, jnp.concatenate([dxs[d] for d in range(TP)], axis=0)).astype(BF16)
    forward_xmate(3)
    for k in range(4):
        collect_x(k)
    h_all = dot(spread, jnp.concatenate([xrecv[d] for d in range(TP)], axis=0))
    for r0 in range(0, TOK, 16):
        h = h_all[r0:r0 + 16, :]
        xh = h * lax.rsqrt(jnp.mean(h * h, axis=-1, keepdims=True) + RMS_EPS)
        y_ref[pl.ds(r0, 16), :] = xh.astype(BF16) * gain
    for i in range(1, TP):
        src = (me + i) % TP
        arrived(dgp_ref.at[src], g_sem.at[src])
    for cp in sends:
        cp.wait_send()


def exchange(ids, table, gain, grad):
    vmem = pl.BlockSpec(memory_space=pltpu.VMEM)
    dma = pltpu.SemaphoreType.DMA
    return pl.pallas_call(
        exchange_kernel,
        out_shape=(
            jax.ShapeDtypeStruct((NC, HID), BF16),
            jax.ShapeDtypeStruct((8, NC), I32),
            jax.ShapeDtypeStruct((TOK, HID), BF16),
            jax.ShapeDtypeStruct((TP, 1, HID), F32),
            jax.ShapeDtypeStruct((1,), I32),
        ),
        in_specs=[vmem, pl.BlockSpec(memory_space=pltpu.HBM), vmem, vmem],
        out_specs=(vmem, vmem, vmem, vmem, pl.BlockSpec(memory_space=pltpu.SMEM)),
        scratch_shapes=[
            pltpu.VMEM((ROWS, HID), BF16),
            dma((CHUNKS,)),
            pltpu.VMEM((4, XC, HID), BF16),
            pltpu.VMEM((TP, XC, HID), BF16),
            pltpu.VMEM((3, DC, HID), BF16),
            pltpu.VMEM((4, DC, HID), BF16),
            pltpu.VMEM((TP, DW, HID), BF16),
            pltpu.VMEM((TP, DW, HID), BF16),
            pltpu.VMEM((1, HID), F32),
            dma((3,)), dma((12,)), dma((TP,)), dma((3,)), dma((4,)), dma((12,)), dma((TP,)), dma((TP - 1,)), dma((TP,)),
        ],
        compiler_params=pltpu.CompilerParams(collective_id=0, has_side_effects=True),
        name='exchange',
    )(ids, table, gain, grad)


BLK = 512
HALF = NC // 2


def finish_kernel(dxc_ref, clid_ref, y_in_ref, dgp_ref, de_ref, y_ref, dg_ref, sem):
    i = pl.program_id(0)
    keep = pltpu.make_async_copy(y_in_ref, y_ref, sem)

    @pl.when(i == 0)
    def _():
        keep.start()

    rows = lax.broadcasted_iota(I32, (BLK, HALF), 0) + i * BLK
    de_ref[...] = dot(one_hot(rows == clid_ref[0:1, :HALF]), dxc_ref[:HALF, :])

    @pl.when(jnp.max(clid_ref[0:1, HALF:]) >= 0)
    def _():
        de_ref[...] += dot(one_hot(rows == clid_ref[0:1, HALF:]), dxc_ref[HALF:, :])

    @pl.when(i == ROWS // BLK - 1)
    def _():
        total = dgp_ref[0]
        for d in range(1, TP):
            total = total + dgp_ref[d]
        dg_ref[...] = total
        keep.wait()


def finish(dxc, clid, y_in, dgp):
    vmem = pl.BlockSpec(memory_space=pltpu.VMEM)
    return pl.pallas_call(
        finish_kernel,
        grid=(ROWS // BLK,),
        out_shape=(
            jax.ShapeDtypeStruct((ROWS, HID), F32),
            jax.ShapeDtypeStruct((TOK, HID), BF16),
            jax.ShapeDtypeStruct((1, HID), F32),
        ),
        in_specs=[vmem] * 4,
        out_specs=(pl.BlockSpec((BLK, HID), lambda i: (i, 0)), pl.BlockSpec(memory_space=pltpu.HBM), vmem),
        scratch_shapes=[pltpu.SemaphoreType.DMA],
        name='finish',
    )(dxc, clid, y_in, dgp)


def swap_kernel(src_ref, dst_ref, local_sem, send_sem, recv_sem):
    me = lax.axis_index('tp')
    barrier = pltpu.get_barrier_semaphore()

    def greet(i, carry):
        pl.semaphore_signal(barrier, inc=1, device_id={'tp': (me + i) % TP}, device_id_type=MESH)
        return carry

    lax.fori_loop(1, TP, greet, 0)
    pl.semaphore_wait(barrier, TP - 1)

    def copy(i):
        peer = (me + i) % TP
        return pltpu.make_async_remote_copy(
            src_ref=src_ref.at[peer], dst_ref=dst_ref.at[me], send_sem=send_sem.at[i], recv_sem=recv_sem.at[me],
            device_id={'tp': peer}, device_id_type=MESH)

    def start(i, carry):
        copy(i).start()
        return carry

    lax.fori_loop(1, TP, start, 0)
    keep = pltpu.make_async_copy(src_ref.at[me], dst_ref.at[me], local_sem)
    keep.start()

    def wait(i, carry):
        peer = (me + i) % TP
        pltpu.make_async_remote_copy(
            src_ref=src_ref.at[peer], dst_ref=dst_ref.at[peer], send_sem=send_sem.at[i], recv_sem=recv_sem.at[peer],
            device_id={'tp': peer}, device_id_type=MESH).wait()
        return carry

    lax.fori_loop(1, TP, wait, 0)
    keep.wait()


def swap(blocks, cid):
    return pl.pallas_call(
        swap_kernel,
        out_shape=jax.ShapeDtypeStruct(blocks.shape, blocks.dtype),
        in_specs=[pl.BlockSpec(memory_space=pl.ANY)],
        out_specs=pl.BlockSpec(memory_space=pl.ANY),
        scratch_shapes=[pltpu.SemaphoreType.DMA, pltpu.SemaphoreType.DMA((TP,)), pltpu.SemaphoreType.DMA((TP,))],
        compiler_params=pltpu.CompilerParams(collective_id=cid, has_side_effects=True),
        name='swap',
    )(blocks)


def general(ids, table, gain, grad):
    local = ids.reshape(-1) - lax.axis_index('tp') * ROWS
    mine = (local >= 0) & (local < ROWS)
    looked = jnp.take(table, jnp.where(mine, local, 0), axis=0)
    parts = swap(jnp.where(mine[:, None], looked, jnp.zeros((), BF16)).reshape(TP, TOK, HID), 1)
    h = jnp.sum(parts.astype(F32), axis=0)
    inv = lax.rsqrt(jnp.mean(h * h, axis=-1, keepdims=True) + RMS_EPS)
    xh = h * inv
    y = xh.astype(BF16) * gain
    gr = grad.astype(F32)
    part = jnp.sum(gr * xh, axis=0)
    u = gr * gain.astype(F32)
    dx = (inv * (u - xh * jnp.mean(u * xh, axis=-1, keepdims=True))).astype(BF16)
    dx_all = swap(jnp.broadcast_to(dx[None], (TP, TOK, HID)), 2).reshape(SEQ, HID)
    dg = jnp.sum(swap(jnp.broadcast_to(part.reshape(1, TOK // 8, 128), (TP, TOK // 8, 128)), 3), axis=0).reshape(1, HID)
    de = jax.ops.segment_sum(dx_all.astype(F32), jnp.where(mine, local, ROWS), num_segments=ROWS)
    return de, y, dg


def device_step(token_ids, table, gain, grad):
    ids = token_ids.reshape(TP, TOK)
    gain = gain.reshape(1, HID)
    grad = grad.reshape(TOK, HID)
    dxc, clid, y_in, dgp, flag = exchange(ids, table, gain, grad)
    de, y, dg = lax.cond(
        flag[0] > 0,
        lambda: general(ids, table, gain, grad),
        lambda: finish(dxc, clid, y_in, dgp),
    )
    return y.reshape(1, TOK, HID), de, dg.reshape(HID)


def solution(mesh):
    return jax.shard_map(
        device_step, mesh=mesh,
        in_specs=(P('dp', None), P('tp', None), P(None), P('dp', 'tp', None)),
        out_specs=(P('dp', 'tp', None), P(('dp', 'tp'), None), P('dp')), check_vma=False)
```

time: 93.1 us -> 67.2 us (0.72)
  the two profiles are of different devices: /device:TPU:1 before, /device:TPU:9 now
where the time goes in v2:
time: 67.2 us; the launch traced here: 66.9 us
  Pallas kernels  63.8 us (95%)
  local copies, waits for them, and re-layouts  1.55 us (2%)
  between operations  1.39 us (2%)
    pallas_call x1, Pallas kernels, exchange(): pl.pallas_call(exchange_kernel, out_shape=(jax.ShapeDtypeStruct((NC, HID)...  52.5 us
    pallas_call x1, Pallas kernels, finish(): pl.pallas_call(finish_kernel, grid=(ROWS // BLK,), out_shape=(jax.ShapeDt...  11.3 us

profile of v2, /device:TPU:9, one launch (start us, length us, event | category | flops | bytes accessed | tf_op | source)
XLA Modules:
  0.0 66.9 jit_solution(6916203920534894920)
XLA Ops:
  0.6 0.0 copy-start.1
  0.6 0.0 copy-start
  0.7 0.8 %reshape.154.gain_ref = bf16[1,2048]{1,0:T(2,128)(2,1)S(1)} reshape(bf16[2048]{0:T(1024)(128)(2,1)} %param.8) | data formatting | bytes 8192 | tf_op jit(solution)/shard_map/reshape | solution.py:489
  1.4 52.5 %exchange.1 = (bf16[512,2048]{1,0:T(8,128)(2,1)}, s32[8,512]{1,0:T(8,128)S(1)}, bf16[128,2048]{1,0:T(8,128)(2,1)S(1)}, f32[16,1,2048]{2,1,0:T(1,128)S(1)}, s32[1]{0:T(128)}) custom-call(s32[16,128]{1,0:T(8,128)} %bitcast.27, bf16[3072,2048]{1,0:T(8,128)(2,1)} %table_ref.1, bf16[1,2048]{1,0:T(2,128)(2,1)S(1)} %reshape.154.gain_ref, bf16[128,2048]{1,0:T(8,128)(2,1)} %bitcast.24), custom_call_target="tpu_custom_call" | custom-call | tf_op jit(solution)/shard_map/exchange/pallas_call | solution.py:347
  54.6 0.0 copy-done.1
  54.6 0.0 copy-done
  54.6 11.5 %conditional.1 = (f32[3072,2048]{1,0:T(8,128)}, bf16[1,128,2048]{2,1,0:T(8,128)(2,1)S(1)}, f32[2048]{0:T(1024)S(1)}) conditional(s32[]{:T(128)} %bitcast.14, (bf16[512,2048]{1,0:T(8,128)(2,1)}, s32[8,512]{1,0:T(8,128)S(1)}, bf16[128,2048]{1,0:T(8,128)(2,1)S(1)}, f32[16,1,2048]{2,1,0:T(1,128)S(1)}) %tuple.20, (s32[1,2048]{1,0:T(1,128)S(1)}, ...), branch_computations={%region_0.0_spmd, %region_1.8_spmd} | conditional | flops 29962372 | bytes 92165192 | solution.py:492
  54.8 11.3 %finish.1 = (f32[3072,2048]{1,0:T(8,128)}, bf16[128,2048]{1,0:T(8,128)(2,1)S(1)}, f32[1,2048]{1,0:T(1,128)S(1)}) custom-call(bf16[512,2048]{1,0:T(8,128)(2,1)} %get-tuple-element.21.dxc_ref, s32[8,512]{1,0:T(8,128)S(1)} %get-tuple-element.22.clid_ref, bf16[128,2048]{1,0:T(8,128)(2,1)S(1)} %get-tuple-element.23.y_in_ref, ...), custom_call_target="tpu_custom_call" | custom-call | tf_op jit(solution)/shard_map/cond/branch_0_fun/finish/pallas_call | solution.py:405
  66.1 0.0 copy-start.2
  66.1 0.0 copy-start.3
  66.1 0.8 %copy-done.2 = bf16[1,128,2048]{2,1,0:T(8,128)(2,1)} copy-done((bf16[1,128,2048]{2,1,0:T(8,128)(2,1)}, bf16[1,128,2048]{2,1,0:T(8,128)(2,1)S(1)}, u32[]{:S(2)}) %copy-start.2) | copy-done | bytes 524312
  66.9 0.0 copy-done.3
Async XLA Ops:
  0.6 54.0 %copy-start.1 = (s32[1,2048]{1,0:T(1,128)S(1)}, s32[1,2048]{1,0:T(1,128)}, u32[]{:S(2)}) copy-start(s32[1,2048]{1,0:T(1,128)} %param.6) | copy-start | bytes 24580
  0.6 54.0 %copy-start = (bf16[1,128,2048]{2,1,0:T(8,128)(2,1)S(1)}, bf16[1,128,2048]{2,1,0:T(8,128)(2,1)}, u32[]{:S(2)}) copy-start(bf16[1,128,2048]{2,1,0:T(8,128)(2,1)} %param.9) | copy-start | bytes 1572868
  66.1 0.8 %copy-start.2 = (bf16[1,128,2048]{2,1,0:T(8,128)(2,1)}, bf16[1,128,2048]{2,1,0:T(8,128)(2,1)S(1)}, u32[]{:S(2)}) copy-start(bf16[1,128,2048]{2,1,0:T(8,128)(2,1)S(1)} %get-tuple-element.40) | copy-start | bytes 1572868
  66.1 0.8 %copy-start.3 = (f32[2048]{0:T(1024)}, f32[2048]{0:T(1024)S(1)}, u32[]{:S(2)}) copy-start(f32[2048]{0:T(1024)S(1)} %get-tuple-element.42) | copy-start | bytes 24580

commit v3 on v2

--- a/solution.py
+++ b/solution.py
@@ -272,7 +272,7 @@
     cl = lax.dot_general(halves, compact, (((1,), (1,)), ((), ())), preferred_element_type=F32)
     clid_ref[...] = jnp.broadcast_to((cl[0:1, :] * 64.0 + cl[1:2, :]).astype(I32) - 1, (8, NC))
 
-    gain = gain_ref[...]
+    gain = gain_ref[...].reshape(1, HID)
     gain_f = gain.astype(F32)
     xlid = jnp.broadcast_to(lid, (4 * XC, 128)).T[0:1, :]
     w_iota = lax.broadcasted_iota(I32, (DW, 128), 0)
@@ -347,10 +347,10 @@
     return pl.pallas_call(
         exchange_kernel,
         out_shape=(
-            jax.ShapeDtypeStruct((NC, HID), BF16),
-            jax.ShapeDtypeStruct((8, NC), I32),
-            jax.ShapeDtypeStruct((TOK, HID), BF16),
-            jax.ShapeDtypeStruct((TP, 1, HID), F32),
+            pltpu.VMEM((NC, HID), BF16),
+            pltpu.VMEM((8, NC), I32),
+            pltpu.VMEM((TOK, HID), BF16),
+            pltpu.VMEM((TP, 1, HID), F32),
             jax.ShapeDtypeStruct((1,), I32),
         ),
         in_specs=[vmem, pl.BlockSpec(memory_space=pltpu.HBM), vmem, vmem],
@@ -367,52 +367,78 @@
             pltpu.VMEM((1, HID), F32),
             dma((3,)), dma((12,)), dma((TP,)), dma((3,)), dma((4,)), dma((12,)), dma((TP,)), dma((TP - 1,)), dma((TP,)),
         ],
-        compiler_params=pltpu.CompilerParams(collective_id=0, has_side_effects=True),
+        compiler_params=pltpu.CompilerParams(collective_id=0, has_side_effects=True, vmem_limit_bytes=44 << 20),
         name='exchange',
     )(ids, table, gain, grad)
 
 
-BLK = 512
+BLK = 128
+SLOTS = 8
 HALF = NC // 2
 
 
-def finish_kernel(dxc_ref, clid_ref, y_in_ref, dgp_ref, de_ref, y_ref, dg_ref, sem):
-    i = pl.program_id(0)
-    keep = pltpu.make_async_copy(y_in_ref, y_ref, sem)
-
-    @pl.when(i == 0)
-    def _():
-        keep.start()
-
-    rows = lax.broadcasted_iota(I32, (BLK, HALF), 0) + i * BLK
-    de_ref[...] = dot(one_hot(rows == clid_ref[0:1, :HALF]), dxc_ref[:HALF, :])
-
-    @pl.when(jnp.max(clid_ref[0:1, HALF:]) >= 0)
-    def _():
-        de_ref[...] += dot(one_hot(rows == clid_ref[0:1, HALF:]), dxc_ref[HALF:, :])
-
-    @pl.when(i == ROWS // BLK - 1)
-    def _():
-        total = dgp_ref[0]
-        for d in range(1, TP):
-            total = total + dgp_ref[d]
-        dg_ref[...] = total
-        keep.wait()
+def finish_kernel(dxc_ref, clid_ref, y_in_ref, dgp_ref, de_ref, y_ref, dg_ref, buf, dg_s, sem, buf_sem):
+    steps = ROWS // BLK
+    keep_y = pltpu.make_async_copy(y_in_ref, y_ref, sem.at[0])
+    keep_y.start()
+    more = jnp.max(clid_ref[0:1, HALF:]) >= 0
+
+    def out(i):
+        slot = lax.rem(i, SLOTS)
+        return pltpu.make_async_copy(buf.at[slot], de_ref.at[pl.ds(pl.multiple_of(i * BLK, BLK), BLK)], buf_sem.at[slot])
+
+    def step(i, carry):
+        @pl.when(i >= SLOTS)
+        def _():
+            out(i - SLOTS).wait()
+
+        slot = lax.rem(i, SLOTS)
+        rows = lax.broadcasted_iota(I32, (BLK, HALF), 0) + i * BLK
+        buf[slot] = dot(one_hot(rows == clid_ref[0:1, :HALF]), dxc_ref[:HALF, :])
+
+        @pl.when(more)
+        def _():
+            buf[slot] += dot(one_hot(rows == clid_ref[0:1, HALF:]), dxc_ref[HALF:, :])
+
+        out(i).start()
+        return carry
+
+    lax.fori_loop(0, steps, step, 0)
+    total = dgp_ref[0]
+    for d in range(1, TP):
+        total = total + dgp_ref[d]
+    dg_s[...] = total
+    keep_dg = pltpu.make_async_copy(dg_s, dg_ref, sem.at[1])
+    keep_dg.start()
+
+    def drain(i, carry):
+        out(i).wait()
+        return carry
+
+    lax.fori_loop(steps - SLOTS, steps, drain, 0)
+    keep_y.wait()
+    keep_dg.wait()
 
 
 def finish(dxc, clid, y_in, dgp):
     vmem = pl.BlockSpec(memory_space=pltpu.VMEM)
+    hbm = pl.BlockSpec(memory_space=pltpu.HBM)
     return pl.pallas_call(
         finish_kernel,
-        grid=(ROWS // BLK,),
         out_shape=(
-            jax.ShapeDtypeStruct((ROWS, HID), F32),
-            jax.ShapeDtypeStruct((TOK, HID), BF16),
-            jax.ShapeDtypeStruct((1, HID), F32),
+            pltpu.HBM((ROWS, HID), F32),
+            pltpu.HBM((TOK, HID), BF16),
+            pltpu.HBM((1, HID), F32),
         ),
         in_specs=[vmem] * 4,
-        out_specs=(pl.BlockSpec((BLK, HID), lambda i: (i, 0)), pl.BlockSpec(memory_space=pltpu.HBM), vmem),
-        scratch_shapes=[pltpu.SemaphoreType.DMA],
+        out_specs=(hbm, hbm, hbm),
+        scratch_shapes=[
+            pltpu.VMEM((SLOTS, BLK, HID), F32),
+            pltpu.VMEM((1, HID), F32),
+            pltpu.SemaphoreType.DMA((2,)),
+            pltpu.SemaphoreType.DMA((SLOTS,)),
+        ],
+        compiler_params=pltpu.CompilerParams(vmem_limit_bytes=24 << 20),
         name='finish',
     )(dxc, clid, y_in, dgp)
 
@@ -486,7 +512,6 @@
 
 def device_step(token_ids, table, gain, grad):
     ids = token_ids.reshape(TP, TOK)
-    gain = gain.reshape(1, HID)
     grad = grad.reshape(TOK, HID)
     dxc, clid, y_in, dgp, flag = exchange(ids, table, gain, grad)
     de, y, dg = lax.cond(

time: 67.2 us -> 62.6 us (0.932)
  Pallas kernels: 63.8 us -> 60.7 us
  local copies, waits for them, and re-layouts: 1.55 us -> 0.01 us
    pallas_call x2, Pallas kernels: 63.8 us -> 60.7 us  [the longest x1 51.7 us: exchange(): pl.pallas_call(exchange_kernel, out_shape=(pltpu.VMEM((NC, HID), BF16), p...]
    unnamed x8 -> x6, local copies, waits for them, and re-layouts: 0.79 us -> 0.01 us
    reshape x1 -> x0, local copies, waits for them, and re-layouts: 0.75 us -> none  [device_step(): gain = gain.reshape(1, HID)]
where the time goes in v3:
time: 62.6 us; the launch traced here: 62.4 us
  Pallas kernels  60.7 us (97%)
  between operations  1.54 us (2%)
    pallas_call x1, Pallas kernels, exchange(): pl.pallas_call(exchange_kernel, out_shape=(pltpu.VMEM((NC, HID), BF16), p...  51.7 us
    pallas_call x1, Pallas kernels, finish(): pl.pallas_call(finish_kernel, out_shape=(pltpu.HBM((ROWS, HID), F32), plt...  8.94 us

profile of v3, /device:TPU:9, one launch (start us, length us, event | category | flops | bytes accessed | tf_op | source)
XLA Modules:
  0.0 62.4 jit_solution(5487167056361544559)
XLA Ops:
  0.6 0.0 copy-start.1
  0.6 0.0 copy-start.2
  0.7 0.0 copy-start
  0.7 51.7 %exchange.1 = (bf16[512,2048]{1,0:T(8,128)(2,1)S(1)}, s32[8,512]{1,0:T(8,128)S(1)}, bf16[128,2048]{1,0:T(8,128)(2,1)S(1)}, f32[16,1,2048]{2,1,0:T(1,128)S(1)}, s32[1]{0:T(128)}) custom-call(s32[16,128]{1,0:T(8,128)} %bitcast.29, bf16[3072,2048]{1,0:T(8,128)(2,1)} %table_ref.1, bf16[2048]{0:T(1024)(128)(2,1)} %gain_ref.1, bf16[128,2048]{1,0:T(8,128)(2,1)} %bitcast.24), custom_call_target="tpu_custom_call" | custom-call | tf_op jit(solution)/shard_map/exchange/pallas_call | solution.py:347
  53.1 0.0 copy-done.1
  53.1 0.0 copy-done.2
  53.1 0.0 copy-done
  53.1 9.1 %conditional.1 = (f32[3072,2048]{1,0:T(8,128)}, bf16[1,128,2048]{2,1,0:T(8,128)(2,1)}, f32[2048]{0:T(1024)}) conditional(s32[]{:T(128)} %bitcast.14, (bf16[512,2048]{1,0:T(8,128)(2,1)S(1)}, s32[8,512]{1,0:T(8,128)S(1)}, bf16[128,2048]{1,0:T(8,128)(2,1)S(1)}, f32[16,1,2048]{2,1,0:T(1,128)S(1)}) %tuple.20, (s32[1,2048]{1,0:T(1,128)S(1)}, ...), branch_computations={%region_0.0_spmd, %region_1.8_spmd} | conditional | flops 29962372 | bytes 92157000 | solution.py:517
  53.3 8.9 %finish.1 = (f32[3072,2048]{1,0:T(8,128)}, bf16[128,2048]{1,0:T(8,128)(2,1)}, f32[1,2048]{1,0:T(1,128)}) custom-call(bf16[512,2048]{1,0:T(8,128)(2,1)S(1)} %get-tuple-element.21.dxc_ref, s32[8,512]{1,0:T(8,128)S(1)} %get-tuple-element.22.clid_ref, bf16[128,2048]{1,0:T(8,128)(2,1)S(1)} %get-tuple-element.23.y_in_ref, f32[16,1,2048]{2,1,0:T(1,128)S(1)} %get-tuple-element.24.dgp_ref), custom_call_target="tpu_custom_call" | custom-call | tf_op jit(solution)/shard_map/cond/branch_0_fun/finish/pallas_call | solution.py:426
Async XLA Ops:
  0.6 52.5 %copy-start.1 = (bf16[2048]{0:T(1024)(128)(2,1)S(1)}, bf16[2048]{0:T(1024)(128)(2,1)}, u32[]{:S(2)}) copy-start(bf16[2048]{0:T(1024)(128)(2,1)} %gain_ref.1) | copy-start | bytes 12292
  0.6 52.5 %copy-start.2 = (s32[1,2048]{1,0:T(1,128)S(1)}, s32[1,2048]{1,0:T(1,128)}, u32[]{:S(2)}) copy-start(s32[1,2048]{1,0:T(1,128)} %param.6) | copy-start | bytes 24580
  0.7 52.5 %copy-start = (bf16[1,128,2048]{2,1,0:T(8,128)(2,1)S(1)}, bf16[1,128,2048]{2,1,0:T(8,128)(2,1)}, u32[]{:S(2)}) copy-start(bf16[1,128,2048]{2,1,0:T(8,128)(2,1)} %param.9) | copy-start | bytes 1572868

commit v4 on v3

--- a/solution.py
+++ b/solution.py
@@ -16,7 +16,7 @@
 XC = 32
 DC = 56
 DW = 40
-NC = 512
+NC = 384
 CHUNKS = 6
 MESH = pl.DeviceIdType.MESH
 F32 = jnp.float32
@@ -42,9 +42,9 @@
 
 
 def exchange_kernel(
-    ids_ref, table_ref, gain_ref, grad_ref,
+    ids_hbm, table_ref, gain_hbm, grad_hbm,
     dxc_ref, clid_ref, y_ref, dgp_ref, flag_ref,
-    tbl, tbl_sem, xs, xrecv, ds, zbuf, drecv, dxs, dgs,
+    ids_ref, gain_ref, grad_ref, in_sem, tbl, tbl_sem, xs, xrecv, ds, zbuf, drecv, dxs, dgs,
     xz_send, xf_send, x_sem, dz_send, z_sem, df_send, d_sem, g_send, g_sem,
 ):
     me = lax.axis_index('tp')
@@ -64,6 +64,12 @@
 
     lax.fori_loop(1, TP, greet, 0)
 
+    first_loads = [
+        pltpu.make_async_copy(src, dst, in_sem.at[i])
+        for i, (src, dst) in enumerate(((ids_hbm, ids_ref), (grad_hbm, grad_ref), (gain_hbm, gain_ref)))
+    ]
+    for load in first_loads:
+        load.start()
     part = ROWS // CHUNKS
     loads = [
         pltpu.make_async_copy(table_ref.at[pl.ds(i * part, part)], tbl.at[pl.ds(i * part, part)], tbl_sem.at[i])
@@ -85,6 +91,7 @@
             src_ref=ref, dst_ref=ref, send_sem=xz_send.at[0], recv_sem=sem,
             device_id={'tp': sib}, device_id_type=MESH).wait_recv()
 
+    first_loads[0].wait()
     ids = ids_ref[...]
     own = owner_of(ids)
     row_iota = lax.broadcasted_iota(I32, (TP, 128), 0)
@@ -127,13 +134,19 @@
             src = zs[k] * 4 + ((1 - y) * 2 if j else y * 2) + (1 - c)
             arrived(drecv.at[src], d_sem.at[src])
 
-    for k in (1, 2, 3):
-        ds[k - 1] = pack_dy(k)
+    def send_dy(k):
+        send(ds.at[k - 1], zbuf.at[k], dz_send.at[k - 1], z_sem.at[k], zs[k] * 4 + lane)
+
+    first_loads[1].wait()
+    first_loads[2].wait()
+    ds[0] = pack_dy(1)
+    pl.semaphore_wait(barrier, TP - 1)
+    send_dy(1)
     zbuf[0] = pack_dy(0)
-    pl.semaphore_wait(barrier, TP - 1)
-    for k in (1, 2, 3):
-        send(ds.at[k - 1], zbuf.at[k], dz_send.at[k - 1], z_sem.at[k], zs[k] * 4 + lane)
     forward_z(0)
+    ds[1] = pack_dy(2)
+    send_dy(2)
+    ds[2] = pack_dy(3)
 
     idc = columns(ids)
     dup_rows = []
@@ -206,6 +219,7 @@
     for k in (1, 2, 3):
         send(xs.at[zs[k]], xrecv.at[me], xz_send.at[k - 1], x_sem.at[me], zs[k] * 4 + lane)
     forward_x(0)
+    send_dy(3)
     forward_z(1)
     forward_zmate(0)
 
@@ -244,15 +258,25 @@
     flag_ref[0] = over
     forward_xmate(0)
 
-    dslot = jnp.where(mine & (drank < DW), jnp.where(y == 0, drank, DW - 1 - drank), -1)
-    dslot_c = columns(dslot)
+    def by_group(rows):
+        out = []
+        for k in range(4):
+            part_k = jnp.zeros((4, 128), I32)
+            for s in range(4):
+                part_k = part_k + jnp.where(zs[k] == s, rows[4 * s:4 * s + 4, :], 0)
+            out.append(part_k)
+        return jnp.concatenate(out, axis=0)
+
+    dslot = by_group(jnp.where(mine & (drank < DW), jnp.where(y == 0, drank, DW - 1 - drank), -1))
+    dlocal = by_group(local)
+    dslot_c = columns(jnp.concatenate([dslot, dlocal], axis=0))
     lrows = []
     for p in range(TP * DW // 128):
         acc = jnp.zeros((128, 128), I32)
         for d in range(TP):
             if d * DW < (p + 1) * 128 and (d + 1) * DW > p * 128:
                 sc = dslot_c[:, d:d + 1]
-                acc = acc + jnp.where((sc >= 0) & (sc + (d * DW - p * 128) == lan), idc[:, d:d + 1] - me * ROWS + 1, 0)
+                acc = acc + jnp.where((sc >= 0) & (sc + (d * DW - p * 128) == lan), dslot_c[:, TP + d:TP + d + 1] + 1, 0)
         lrows.append(jnp.sum(acc, axis=0, keepdims=True))
     lid1 = jnp.concatenate(lrows + [jnp.zeros((8 - len(lrows), 128), I32)], axis=0)
     has = lid1 > 0
@@ -280,60 +304,73 @@
 
     steps = [(r0, min(16, DW - r0)) for r0 in range(0, DW, 16)]
 
-    def dx_rows(zk, dy_of, gain_sum):
-        pick_row = jnp.where(x_group == zk, xlid, -2)
-        for block, at in dy_of:
-            slot_row = jnp.sum(jnp.where(row_iota == at, dslot, 0), axis=0, keepdims=True)
-            local_row = jnp.sum(jnp.where(row_iota == at, local, 0), axis=0, keepdims=True)
-            dlid = jnp.sum(jnp.where(w_iota == slot_row, local_row + 1, 0), axis=1, keepdims=True) - 1
-            h_all = dot(one_hot(dlid == pick_row), jnp.concatenate([xs[s] for s in range(4)], axis=0))
-            for r0, n in steps:
-                h = h_all[r0:r0 + n, :]
-                inv = lax.rsqrt(jnp.mean(h * h, axis=-1, keepdims=True) + RMS_EPS)
-                xh = h * inv
-                gr = block(r0, n).astype(F32)
-                gain_sum = gain_sum + jnp.sum(gr * xh, axis=0, keepdims=True)
-                u = gr * gain_f
-                dx = inv * (u - xh * jnp.mean(u * xh, axis=-1, keepdims=True))
-                dxs[at, pl.ds(r0, n), :] = dx.astype(BF16)
-        return gain_sum
-
-    def process(k, gain_sum):
+    def dx_block(k, off, block):
+        at = 4 * k + off
+        slot_row = jnp.sum(jnp.where(row_iota == at, dslot, 0), axis=0, keepdims=True)
+        local_row = jnp.sum(jnp.where(row_iota == at, dlocal, 0), axis=0, keepdims=True)
+        dlid = jnp.sum(jnp.where(w_iota == slot_row, local_row + 1, 0), axis=1, keepdims=True) - 1
+        pick = one_hot(dlid == jnp.where(x_group == zs[k], xlid, -2))
+        h_all = dot(pick, jnp.concatenate([xs[s] for s in range(4)], axis=0))
+        for r0, n in steps:
+            h = h_all[r0:r0 + n, :]
+            inv = lax.rsqrt(jnp.mean(h * h, axis=-1, keepdims=True) + RMS_EPS)
+            xh = h * inv
+            u = block(r0, n).astype(F32) * gain_f
+            dx = inv * (u - xh * jnp.mean(u * xh, axis=-1, keepdims=True))
+            dxs[at, pl.ds(r0, n), :] = dx.astype(BF16)
+
+    def own_block(k):
+        dx_block(k, lane, lambda r0, n: zbuf[k, pl.ds(pl.multiple_of(lo + r0, 8), n), :])
+
+    def got_block(k, off):
+        at = zs[k] * 4 + off
+        dx_block(k, off, lambda r0, n: drecv[at, pl.ds(r0, n), :])
+
+    mate_off, sib_off, far_off = (1 - y) * 2 + c, y * 2 + (1 - c), (1 - y) * 2 + (1 - c)
+
+    def process(k):
+        own_block(k)
+        got_block(k, mate_off)
         collect_dy(k)
-        zk = zs[k]
-        out = [(lambda r0, n: zbuf[k, pl.ds(pl.multiple_of(lo + r0, 8), n), :], zk * 4 + lane)]
-        for off in ((1 - y) * 2 + c, y * 2 + (1 - c), (1 - y) * 2 + (1 - c)):
-            at = zk * 4 + off
-            out.append((lambda r0, n, at=at: drecv[at, pl.ds(r0, n), :], at))
-        return dx_rows(zk, out, gain_sum)
+        got_block(k, sib_off)
+        got_block(k, far_off)
 
     forward_z(2)
     forward_zmate(1)
-    gain_sum = process(0, jnp.zeros((1, HID), F32))
-    forward_z(3)
+    process(0)
+    forward_x(1)
     forward_zmate(2)
-    gain_sum = process(1, gain_sum)
-    forward_x(1)
-    forward_zmate(3)
-    gain_sum = process(2, gain_sum)
+    process(1)
     forward_x(2)
     forward_xmate(1)
-    gain_sum = process(3, gain_sum)
+    process(2)
+    forward_x(3)
+    forward_xmate(2)
+    early = 12 * DW
+    dxc_ref[...] = dot(compact[:, :early], jnp.concatenate([dxs[d] for d in range(12)], axis=0)).astype(BF16)
+    forward_z(3)
+    forward_xmate(3)
+    own_block(3)
+    for k in range(4):
+        collect_x(k)
+    h_all = dot(spread, jnp.concatenate([xrecv[d] for d in range(TP)], axis=0))
+    gain_sum = jnp.zeros((1, HID), F32)
+    for r0 in range(0, TOK, 16):
+        h = h_all[r0:r0 + 16, :]
+        xh = h * lax.rsqrt(jnp.mean(h * h, axis=-1, keepdims=True) + RMS_EPS)
+        y_ref[pl.ds(r0, 16), :] = xh.astype(BF16) * gain
+        gain_sum = gain_sum + jnp.sum(grad_ref[pl.ds(r0, 16), :].astype(F32) * xh, axis=0, keepdims=True)
     dgs[...] = gain_sum
     dgp_ref[me] = gain_sum
     for i in range(1, TP):
         send(dgs, dgp_ref.at[me], g_send.at[i - 1], g_sem.at[me], (me + i) % TP)
-    forward_x(3)
-    forward_xmate(2)
-    dxc_ref[...] = dot(compact, jnp.concatenate([dxs[d] for d in range(TP)], axis=0)).astype(BF16)
-    forward_xmate(3)
-    for k in range(4):
-        collect_x(k)
-    h_all = dot(spread, jnp.concatenate([xrecv[d] for d in range(TP)], axis=0))
-    for r0 in range(0, TOK, 16):
-        h = h_all[r0:r0 + 16, :]
-        xh = h * lax.rsqrt(jnp.mean(h * h, axis=-1, keepdims=True) + RMS_EPS)
-        y_ref[pl.ds(r0, 16), :] = xh.astype(BF16) * gain
+    forward_zmate(3)
+    got_block(3, mate_off)
+    collect_dy(3)
+    got_block(3, sib_off)
+    got_block(3, far_off)
+    late = dot(compact[:, early:], jnp.concatenate([dxs[d] for d in range(12, TP)], axis=0))
+    dxc_ref[...] += late.astype(BF16)
     for i in range(1, TP):
         src = (me + i) % TP
         arrived(dgp_ref.at[src], g_sem.at[src])
@@ -351,11 +388,15 @@
             pltpu.VMEM((8, NC), I32),
             pltpu.VMEM((TOK, HID), BF16),
             pltpu.VMEM((TP, 1, HID), F32),
-            jax.ShapeDtypeStruct((1,), I32),
+            pltpu.SMEM((1,), I32),
         ),
-        in_specs=[vmem, pl.BlockSpec(memory_space=pltpu.HBM), vmem, vmem],
+        in_specs=[pl.BlockSpec(memory_space=pltpu.HBM)] * 4,
         out_specs=(vmem, vmem, vmem, vmem, pl.BlockSpec(memory_space=pltpu.SMEM)),
         scratch_shapes=[
+            pltpu.VMEM((TP, TOK), I32),
+            pltpu.VMEM((HID,), BF16),
+            pltpu.VMEM((TOK, HID), BF16),
+            dma((3,)),
             pltpu.VMEM((ROWS, HID), BF16),
             dma((CHUNKS,)),
             pltpu.VMEM((4, XC, HID), BF16),
@@ -374,7 +415,7 @@
 
 BLK = 128
 SLOTS = 8
-HALF = NC // 2
+HALF = 256
 
 
 def finish_kernel(dxc_ref, clid_ref, y_in_ref, dgp_ref, de_ref, y_ref, dg_ref, buf, dg_s, sem, buf_sem):
@@ -398,7 +439,7 @@
 
         @pl.when(more)
         def _():
-            buf[slot] += dot(one_hot(rows == clid_ref[0:1, HALF:]), dxc_ref[HALF:, :])
+            buf[slot] += dot(one_hot(rows[:, :NC - HALF] == clid_ref[0:1, HALF:]), dxc_ref[HALF:, :])
 
         out(i).start()
         return carry

time: 62.6 us -> 59.5 us (0.950)
  Pallas kernels: 60.7 us -> 58.2 us
  between operations: 1.54 us -> 0.87 us
    pallas_call x1, Pallas kernels: 51.7 us -> 49.3 us  [exchange(): pl.pallas_call(exchange_kernel, out_shape=(pltpu.VMEM((NC, HID), BF16), p...]
where the time goes in v4:
time: 59.5 us; the launch traced here: 59.3 us
  Pallas kernels  58.2 us (98%)
  between operations  0.87 us (1%)
    pallas_call x1, Pallas kernels, exchange(): pl.pallas_call(exchange_kernel, out_shape=(pltpu.VMEM((NC, HID), BF16), p...  49.3 us
    pallas_call x1, Pallas kernels, finish(): pl.pallas_call(finish_kernel, out_shape=(pltpu.HBM((ROWS, HID), F32), plt...  8.94 us

profile of v4, /device:TPU:9, one launch (start us, length us, event | category | flops | bytes accessed | tf_op | source)
XLA Modules:
  0.0 59.3 jit_solution(18116262555931359216)
XLA Ops:
  0.6 0.0 copy-start.1
  0.6 0.0 copy-start.2
  0.7 0.0 copy-start
  0.7 49.3 %exchange.1 = (bf16[384,2048]{1,0:T(8,128)(2,1)S(1)}, s32[8,384]{1,0:T(8,128)S(1)}, bf16[128,2048]{1,0:T(8,128)(2,1)S(1)}, f32[16,1,2048]{2,1,0:T(1,128)S(1)}, s32[1]{0:T(128)S(4)}) custom-call(s32[16,128]{1,0:T(8,128)} %bitcast.29, bf16[3072,2048]{1,0:T(8,128)(2,1)} %table_ref.1, bf16[2048]{0:T(1024)(128)(2,1)} %gain_hbm.1, bf16[128,2048]{1,0:T(8,128)(2,1)} %bitcast.24), custom_call_target="tpu_custom_call" | custom-call | tf_op jit(solution)/shard_map/exchange/pallas_call | solution.py:384
  49.9 0.0 copy-done.1
  49.9 0.0 copy-done.2
  50.0 0.0 copy-done
  50.0 9.2 %conditional.1 = (f32[3072,2048]{1,0:T(8,128)}, bf16[1,128,2048]{2,1,0:T(8,128)(2,1)}, f32[2048]{0:T(1024)}) conditional(s32[]{:T(128)} %bitcast.14, (bf16[384,2048]{1,0:T(8,128)(2,1)S(1)}, s32[8,384]{1,0:T(8,128)S(1)}, bf16[128,2048]{1,0:T(8,128)(2,1)S(1)}, f32[16,1,2048]{2,1,0:T(1,128)S(1)}) %tuple.20, (s32[1,2048]{1,0:T(1,128)S(1)}, ...), branch_computations={%region_0.0_spmd, %region_1.8_spmd} | conditional | flops 29962372 | bytes 92157000 | solution.py:558
  50.0 8.9 %finish.1 = (f32[3072,2048]{1,0:T(8,128)}, bf16[128,2048]{1,0:T(8,128)(2,1)}, f32[1,2048]{1,0:T(1,128)}) custom-call(bf16[384,2048]{1,0:T(8,128)(2,1)S(1)} %get-tuple-element.21.dxc_ref, s32[8,384]{1,0:T(8,128)S(1)} %get-tuple-element.22.clid_ref, bf16[128,2048]{1,0:T(8,128)(2,1)S(1)} %get-tuple-element.23.y_in_ref, f32[16,1,2048]{2,1,0:T(1,128)S(1)} %get-tuple-element.24.dgp_ref), custom_call_target="tpu_custom_call" | custom-call | tf_op jit(solution)/shard_map/cond/branch_0_fun/finish/pallas_call | solution.py:467
Async XLA Ops:
  0.6 49.3 %copy-start.1 = (bf16[2048]{0:T(1024)(128)(2,1)S(1)}, bf16[2048]{0:T(1024)(128)(2,1)}, u32[]{:S(2)}) copy-start(bf16[2048]{0:T(1024)(128)(2,1)} %gain_hbm.1) | copy-start | bytes 12292
  0.6 49.3 %copy-start.2 = (s32[1,2048]{1,0:T(1,128)S(1)}, s32[1,2048]{1,0:T(1,128)}, u32[]{:S(2)}) copy-start(s32[1,2048]{1,0:T(1,128)} %param.6) | copy-start | bytes 24580
  0.7 49.3 %copy-start = (bf16[1,128,2048]{2,1,0:T(8,128)(2,1)S(1)}, bf16[1,128,2048]{2,1,0:T(8,128)(2,1)}, u32[]{:S(2)}) copy-start(bf16[1,128,2048]{2,1,0:T(8,128)(2,1)} %param.9) | copy-start | bytes 1572868

commit v5 on v4

--- a/solution.py
+++ b/solution.py
@@ -44,7 +44,7 @@
 def exchange_kernel(
     ids_hbm, table_ref, gain_hbm, grad_hbm,
     dxc_ref, clid_ref, y_ref, dgp_ref, flag_ref,
-    ids_ref, gain_ref, grad_ref, in_sem, tbl, tbl_sem, xs, xrecv, ds, zbuf, drecv, dxs, dgs,
+    ids_ref, gain_ref, grad_ref, in_sem, tbl, tbl_sem, xs, xrecv, ds, zbuf, drecv, dxs, dgs, hs,
     xz_send, xf_send, x_sem, dz_send, z_sem, df_send, d_sem, g_send, g_sem,
 ):
     me = lax.axis_index('tp')
@@ -56,20 +56,20 @@
     ymate = z * 4 + (1 - y) * 2 + c
     zs = [z, z + 1 - 2 * (z % 2), z + 2 - 4 * (z // 2), 3 - z]
 
-    barrier = pltpu.get_barrier_semaphore()
-
-    def greet(i, carry):
-        pl.semaphore_signal(barrier, inc=1, device_id={'tp': (me + i) % TP}, device_id_type=MESH)
-        return carry
-
-    lax.fori_loop(1, TP, greet, 0)
-
     first_loads = [
         pltpu.make_async_copy(src, dst, in_sem.at[i])
         for i, (src, dst) in enumerate(((ids_hbm, ids_ref), (grad_hbm, grad_ref), (gain_hbm, gain_ref)))
     ]
     for load in first_loads:
         load.start()
+    barrier = pltpu.get_barrier_semaphore()
+
+    def greet(i, carry):
+        pl.semaphore_signal(barrier, inc=1, device_id={'tp': (me + i) % TP}, device_id_type=MESH)
+        return carry
+
+    lax.fori_loop(1, TP, greet, 0)
+
     part = ROWS // CHUNKS
     loads = [
         pltpu.make_async_copy(table_ref.at[pl.ds(i * part, part)], tbl.at[pl.ds(i * part, part)], tbl_sem.at[i])
@@ -235,12 +235,14 @@
     mine_c = columns(jnp.concatenate([tslot, slab(ids), jnp.broadcast_to(my_row(ids), (8, 128))], axis=0))
     my_ids_c = mine_c[:, 8:9]
     spread = []
-    for q in range(4):
+    for k in range(4):
         acc = jnp.zeros((128, 128), I32)
         for a in range(4):
-            acc = acc + jnp.where(mine_c[:, a:a + 1] == lan + q * 128, mine_c[:, 4 + a:5 + a] + 1, 0)
+            acc = acc + jnp.where(mine_c[:, a:a + 1] == lan + zs[k] * 128, mine_c[:, 4 + a:5 + a] + 1, 0)
         spread.append(one_hot(my_ids_c == jnp.sum(acc, axis=0, keepdims=True) - 1))
-    spread = jnp.concatenate(spread, axis=1)
+
+    def slab_rows(k):
+        return [xrecv[zs[k] * 4 + j] for j in range(4)]
 
     chip_c = ((idc >> 10) * 171) >> 10
     chip = own >> 1
@@ -346,14 +348,13 @@
     process(2)
     forward_x(3)
     forward_xmate(2)
-    early = 12 * DW
-    dxc_ref[...] = dot(compact[:, :early], jnp.concatenate([dxs[d] for d in range(12)], axis=0)).astype(BF16)
     forward_z(3)
+    for k in range(3):
+        collect_x(k)
+    hs[...] = dot(jnp.concatenate(spread[:3], axis=1), jnp.concatenate(slab_rows(0) + slab_rows(1) + slab_rows(2), axis=0))
     forward_xmate(3)
-    own_block(3)
-    for k in range(4):
-        collect_x(k)
-    h_all = dot(spread, jnp.concatenate([xrecv[d] for d in range(TP)], axis=0))
+    collect_x(3)
+    h_all = hs[...] + dot(spread[3], jnp.concatenate(slab_rows(3), axis=0))
     gain_sum = jnp.zeros((1, HID), F32)
     for r0 in range(0, TOK, 16):
         h = h_all[r0:r0 + 16, :]
@@ -364,6 +365,9 @@
     dgp_ref[me] = gain_sum
     for i in range(1, TP):
         send(dgs, dgp_ref.at[me], g_send.at[i - 1], g_sem.at[me], (me + i) % TP)
+    own_block(3)
+    early = 12 * DW
+    dxc_ref[...] = dot(compact[:, :early], jnp.concatenate([dxs[d] for d in range(12)], axis=0)).astype(BF16)
     forward_zmate(3)
     got_block(3, mate_off)
     collect_dy(3)
@@ -406,6 +410,7 @@
             pltpu.VMEM((TP, DW, HID), BF16),
             pltpu.VMEM((TP, DW, HID), BF16),
             pltpu.VMEM((1, HID), F32),
+            pltpu.VMEM((TOK, HID), F32),
             dma((3,)), dma((12,)), dma((TP,)), dma((3,)), dma((4,)), dma((12,)), dma((TP,)), dma((TP - 1,)), dma((TP,)),
         ],
         compiler_params=pltpu.CompilerParams(collective_id=0, has_side_effects=True, vmem_limit_bytes=44 << 20),

time: 59.5 us -> 56.4 us (0.948)
  Pallas kernels: 58.2 us -> 55 us
    pallas_call x1, Pallas kernels: 49.3 us -> 46 us  [exchange(): pl.pallas_call(exchange_kernel, out_shape=(pltpu.VMEM((NC, HID), BF16), p...]
where the time goes in v5:
time: 56.4 us; the launch traced here: 56 us
  Pallas kernels  55 us (98%)
  between operations  0.85 us (2%)
    pallas_call x1, Pallas kernels, exchange(): pl.pallas_call(exchange_kernel, out_shape=(pltpu.VMEM((NC, HID), BF16), p...  46 us
    pallas_call x1, Pallas kernels, finish(): pl.pallas_call(finish_kernel, out_shape=(pltpu.HBM((ROWS, HID), F32), plt...  8.93 us

profile of v5, /device:TPU:9, one launch (start us, length us, event | category | flops | bytes accessed | tf_op | source)
XLA Modules:
  0.0 56.0 jit_solution(455115037059347239)
XLA Ops:
  0.6 0.0 copy-start.1
  0.6 0.0 copy-start.2
  0.7 0.0 copy-start
  0.7 46.0 %exchange.1 = (bf16[384,2048]{1,0:T(8,128)(2,1)S(1)}, s32[8,384]{1,0:T(8,128)S(1)}, bf16[128,2048]{1,0:T(8,128)(2,1)S(1)}, f32[16,1,2048]{2,1,0:T(1,128)S(1)}, s32[1]{0:T(128)S(4)}) custom-call(s32[16,128]{1,0:T(8,128)} %bitcast.29, bf16[3072,2048]{1,0:T(8,128)(2,1)} %table_ref.1, bf16[2048]{0:T(1024)(128)(2,1)} %gain_hbm.1, bf16[128,2048]{1,0:T(8,128)(2,1)} %bitcast.24), custom_call_target="tpu_custom_call" | custom-call | tf_op jit(solution)/shard_map/exchange/pallas_call | solution.py:388
  46.7 0.0 copy-done.1
  46.7 0.0 copy-done.2
  46.7 0.0 copy-done
  46.7 9.1 %conditional.1 = (f32[3072,2048]{1,0:T(8,128)}, bf16[1,128,2048]{2,1,0:T(8,128)(2,1)}, f32[2048]{0:T(1024)}) conditional(s32[]{:T(128)} %bitcast.14, (bf16[384,2048]{1,0:T(8,128)(2,1)S(1)}, s32[8,384]{1,0:T(8,128)S(1)}, bf16[128,2048]{1,0:T(8,128)(2,1)S(1)}, f32[16,1,2048]{2,1,0:T(1,128)S(1)}) %tuple.20, (s32[1,2048]{1,0:T(1,128)S(1)}, ...), branch_computations={%region_0.0_spmd, %region_1.8_spmd} | conditional | flops 29962372 | bytes 92157000 | solution.py:563
  46.7 8.9 %finish.1 = (f32[3072,2048]{1,0:T(8,128)}, bf16[128,2048]{1,0:T(8,128)(2,1)}, f32[1,2048]{1,0:T(1,128)}) custom-call(bf16[384,2048]{1,0:T(8,128)(2,1)S(1)} %get-tuple-element.21.dxc_ref, s32[8,384]{1,0:T(8,128)S(1)} %get-tuple-element.22.clid_ref, bf16[128,2048]{1,0:T(8,128)(2,1)S(1)} %get-tuple-element.23.y_in_ref, f32[16,1,2048]{2,1,0:T(1,128)S(1)} %get-tuple-element.24.dgp_ref), custom_call_target="tpu_custom_call" | custom-call | tf_op jit(solution)/shard_map/cond/branch_0_fun/finish/pallas_call | solution.py:472
Async XLA Ops:
  0.6 46.1 %copy-start.1 = (bf16[2048]{0:T(1024)(128)(2,1)S(1)}, bf16[2048]{0:T(1024)(128)(2,1)}, u32[]{:S(2)}) copy-start(bf16[2048]{0:T(1024)(128)(2,1)} %gain_hbm.1) | copy-start | bytes 12292
  0.6 46.1 %copy-start.2 = (s32[1,2048]{1,0:T(1,128)S(1)}, s32[1,2048]{1,0:T(1,128)}, u32[]{:S(2)}) copy-start(s32[1,2048]{1,0:T(1,128)} %param.6) | copy-start | bytes 24580
  0.7 46.1 %copy-start = (bf16[1,128,2048]{2,1,0:T(8,128)(2,1)S(1)}, bf16[1,128,2048]{2,1,0:T(8,128)(2,1)}, u32[]{:S(2)}) copy-start(bf16[1,128,2048]{2,1,0:T(8,128)(2,1)} %param.9) | copy-start | bytes 1572868

commit v6 on v5

--- a/solution.py
+++ b/solution.py
@@ -219,6 +219,7 @@
     for k in (1, 2, 3):
         send(xs.at[zs[k]], xrecv.at[me], xz_send.at[k - 1], x_sem.at[me], zs[k] * 4 + lane)
     forward_x(0)
+    late_send = len(sends)
     send_dy(3)
     forward_z(1)
     forward_zmate(0)
@@ -348,6 +349,7 @@
     process(2)
     forward_x(3)
     forward_xmate(2)
+    settled = len(sends)
     forward_z(3)
     for k in range(3):
         collect_x(k)
@@ -368,18 +370,23 @@
     own_block(3)
     early = 12 * DW
     dxc_ref[...] = dot(compact[:, :early], jnp.concatenate([dxs[d] for d in range(12)], axis=0)).astype(BF16)
+    arrived(drecv.at[zs[3] * 4 + sib_off], d_sem.at[zs[3] * 4 + sib_off])
+    got_block(3, sib_off)
+    for i, cp in enumerate(sends[:settled]):
+        if i != late_send:
+            cp.wait_send()
     forward_zmate(3)
     got_block(3, mate_off)
-    collect_dy(3)
-    got_block(3, sib_off)
+    arrived(drecv.at[zs[3] * 4 + far_off], d_sem.at[zs[3] * 4 + far_off])
     got_block(3, far_off)
     late = dot(compact[:, early:], jnp.concatenate([dxs[d] for d in range(12, TP)], axis=0))
     dxc_ref[...] += late.astype(BF16)
     for i in range(1, TP):
         src = (me + i) % TP
         arrived(dgp_ref.at[src], g_sem.at[src])
-    for cp in sends:
-        cp.wait_send()
+    for i, cp in enumerate(sends):
+        if i >= settled or i == late_send:
+            cp.wait_send()
 
 
 def exchange(ids, table, gain, grad):

time: 56.4 us -> 56.3 us (level)
  no operation moved by 1% of the time
where the time goes in v6:
time: 56.3 us; the launch traced here: 55.9 us
  Pallas kernels  54.8 us (97%)
  between operations  0.85 us (2%)
    pallas_call x1, Pallas kernels, exchange(): pl.pallas_call(exchange_kernel, out_shape=(pltpu.VMEM((NC, HID), BF16), p...  45.9 us
    pallas_call x1, Pallas kernels, finish(): pl.pallas_call(finish_kernel, out_shape=(pltpu.HBM((ROWS, HID), F32), plt...  8.94 us

profile of v6, /device:TPU:9, one launch (start us, length us, event | category | flops | bytes accessed | tf_op | source)
XLA Modules:
  0.0 55.9 jit_solution(13789363238577265452)
XLA Ops:
  0.6 0.0 copy-start.1
  0.6 0.0 copy-start.2
  0.7 0.0 copy-start
  0.7 45.9 %exchange.1 = (bf16[384,2048]{1,0:T(8,128)(2,1)S(1)}, s32[8,384]{1,0:T(8,128)S(1)}, bf16[128,2048]{1,0:T(8,128)(2,1)S(1)}, f32[16,1,2048]{2,1,0:T(1,128)S(1)}, s32[1]{0:T(128)S(4)}) custom-call(s32[16,128]{1,0:T(8,128)} %bitcast.29, bf16[3072,2048]{1,0:T(8,128)(2,1)} %table_ref.1, bf16[2048]{0:T(1024)(128)(2,1)} %gain_hbm.1, bf16[128,2048]{1,0:T(8,128)(2,1)} %bitcast.24), custom_call_target="tpu_custom_call" | custom-call | tf_op jit(solution)/shard_map/exchange/pallas_call | solution.py:395
  46.6 0.0 copy-done.1
  46.6 0.0 copy-done.2
  46.6 0.0 copy-done
  46.6 9.1 %conditional.1 = (f32[3072,2048]{1,0:T(8,128)}, bf16[1,128,2048]{2,1,0:T(8,128)(2,1)}, f32[2048]{0:T(1024)}) conditional(s32[]{:T(128)} %bitcast.14, (bf16[384,2048]{1,0:T(8,128)(2,1)S(1)}, s32[8,384]{1,0:T(8,128)S(1)}, bf16[128,2048]{1,0:T(8,128)(2,1)S(1)}, f32[16,1,2048]{2,1,0:T(1,128)S(1)}) %tuple.20, (s32[1,2048]{1,0:T(1,128)S(1)}, ...), branch_computations={%region_0.0_spmd, %region_1.8_spmd} | conditional | flops 29962372 | bytes 92157000 | solution.py:570
  46.8 8.9 %finish.1 = (f32[3072,2048]{1,0:T(8,128)}, bf16[128,2048]{1,0:T(8,128)(2,1)}, f32[1,2048]{1,0:T(1,128)}) custom-call(bf16[384,2048]{1,0:T(8,128)(2,1)S(1)} %get-tuple-element.21.dxc_ref, s32[8,384]{1,0:T(8,128)S(1)} %get-tuple-element.22.clid_ref, bf16[128,2048]{1,0:T(8,128)(2,1)S(1)} %get-tuple-element.23.y_in_ref, f32[16,1,2048]{2,1,0:T(1,128)S(1)} %get-tuple-element.24.dgp_ref), custom_call_target="tpu_custom_call" | custom-call | tf_op jit(solution)/shard_map/cond/branch_0_fun/finish/pallas_call | solution.py:479
Async XLA Ops:
  0.6 46.0 %copy-start.1 = (bf16[2048]{0:T(1024)(128)(2,1)S(1)}, bf16[2048]{0:T(1024)(128)(2,1)}, u32[]{:S(2)}) copy-start(bf16[2048]{0:T(1024)(128)(2,1)} %gain_hbm.1) | copy-start | bytes 12292
  0.6 46.0 %copy-start.2 = (s32[1,2048]{1,0:T(1,128)S(1)}, s32[1,2048]{1,0:T(1,128)}, u32[]{:S(2)}) copy-start(s32[1,2048]{1,0:T(1,128)} %param.6) | copy-start | bytes 24580
  0.7 46.0 %copy-start = (bf16[1,128,2048]{2,1,0:T(8,128)(2,1)S(1)}, bf16[1,128,2048]{2,1,0:T(8,128)(2,1)}, u32[]{:S(2)}) copy-start(bf16[1,128,2048]{2,1,0:T(8,128)(2,1)} %param.9) | copy-start | bytes 1572868
